TPU v7x, 32 devices: a whole 2x2x4 slice. The times are simulated.
32 devices in a mesh: gx: 4 (over z), gy: 4 (over x, core), ens: 2 (over y).
Axes of the slice: x: 2, y: 2, z: 4, core: 2. Of those that a mesh axis runs over, the one named last changes fastest.
Arguments:
- state: float32 [128, 64, 512], P('ens', 'gy', 'gx'), may hold values from -6 to 6
- u_vel: float32 [64, 512], P('gy', 'gx'), may hold values from -0.4 to 0.4
- v_vel: float32 [64, 512], P('gy', 'gx'), may hold values from -0.4 to 0.4
- land: int32 [64, 512], P('gy', 'gx'), may hold values 0 or 1
- forcing: float32 [8, 64, 512], P(None, 'gy', 'gx'), may hold values from -3 to 3
- member_mode: int32 [128], P('ens'), may hold values from 0 to 7
- theta: float32 [128, 4], P('ens'), may hold values from -1 to 1
- obs_index: int32 [4, 4, 128], P('gy', 'gx'), may hold values from 0 to 2047
- obs_values: float32 [4, 4, 128], P('gy', 'gx'), may hold values from -6 to 6
- obs_sigma: float32 [4, 4, 128], P('gy', 'gx'), may hold values from 0.5 to 4
Outputs:
- final_state: float32 [128, 64, 512], P('ens', 'gy', 'gx')
- new_theta: float32 [128, 4], P('ens')
All inputs are finite; a program needn't handle non-finite values. No bound on the sum of `land` on one device may be relied on, other than what follows from the above.
Results may differ from a plain program's by a relative error of at most 0.0003.
Values sent between devices are 32-bit elements; how exact they have to be, the bound alone decides.
A program may use at most 64 MiB of HBM per device.

v0:
```python
import functools
import jax
import jax.numpy as jnp
from jax import lax
from jax.experimental import pallas as pl
from jax.experimental.pallas import tpu as pltpu
from jax.sharding import PartitionSpec as P

STEPS = 4
DEPTH = 2 * STEPS
F32 = jnp.float32
VM = pltpu.VMEM
MESH = pl.DeviceIdType.MESH
HIGH = lax.Precision.HIGHEST


def vspec():
    return pl.BlockSpec(memory_space=pltpu.VMEM)


def halo_kernel(n_gx, n_gy, q_ref, forcing_ref, u_ref, v_ref, land_ref, f_ref, qt_ref, qb_ref, ft_ref, fb_ref, mid_ref, top_ref, bot_ref,
                pack, row_send, row_recv, gx_send, gx_recv, gy_send, gy_recv):
    gx, gy = lax.axis_index("gx"), lax.axis_index("gy")
    right, left = lax.rem(gx + 1, n_gx), lax.rem(gx + n_gx - 1, n_gx)
    has_up, has_down = gy > 0, gy < n_gy - 1
    up, down = jnp.maximum(gy - 1, 0), jnp.minimum(gy + 1, n_gy - 1)
    members, rows, cols = q_ref.shape
    fields = f_ref.shape[0]

    patterns = forcing_ref.shape[0]
    f_ref[0:patterns] = forcing_ref[...]
    f_ref[patterns] = u_ref[...]
    f_ref[patterns + 1] = v_ref[...]
    f_ref[patterns + 2] = (1 - land_ref[...]).astype(F32)
    f_ref[patterns + 3:] = jnp.zeros((fields - patterns - 3, rows, cols), F32)

    barrier = pltpu.get_barrier_semaphore()
    pl.semaphore_signal(barrier, inc=1, device_id={"gx": right}, device_id_type=MESH)
    pl.semaphore_signal(barrier, inc=1, device_id={"gx": left}, device_id_type=MESH)

    @pl.when(has_up)
    def _():
        pl.semaphore_signal(barrier, inc=1, device_id={"gy": up}, device_id_type=MESH)

    @pl.when(has_down)
    def _():
        pl.semaphore_signal(barrier, inc=1, device_id={"gy": down}, device_id_type=MESH)

    lane = lax.broadcasted_iota(jnp.int32, (8, cols), 1)

    def pack_from(ref, base):
        def body(g, carry):
            lo = jnp.zeros((8, cols), F32)
            hi = jnp.zeros((8, cols), F32)
            for r in range(rows):
                val = ref[pl.ds(g * 8, 8), r, :]
                mine = (lane // DEPTH) == r
                hi = jnp.where(mine, pltpu.roll(val, (r * DEPTH + DEPTH) % cols, 1), hi)
                lo = jnp.where(mine, pltpu.roll(val, (r * DEPTH) % cols, 1), lo)
            pack[0, pl.ds(base + g * 8, 8), :] = hi
            pack[1, pl.ds(base + g * 8, 8), :] = lo
            return carry
        lax.fori_loop(0, ref.shape[0] // 8, body, 0)

    pl.semaphore_wait(barrier, 2 + has_up.astype(jnp.int32) + has_down.astype(jnp.int32))

    def rdma(src, dst, send, recv, dev):
        return pltpu.make_async_remote_copy(src_ref=src, dst_ref=dst, send_sem=send, recv_sem=recv,
                                            device_id=dev, device_id_type=MESH)

    downs = [rdma(q_ref.at[:, rows - DEPTH:, :], qt_ref, row_send.at[0], row_recv.at[0], {"gy": down}),
             rdma(f_ref.at[:, rows - DEPTH:, :], ft_ref, row_send.at[1], row_recv.at[1], {"gy": down})]
    ups = [rdma(q_ref.at[:, :DEPTH, :], qb_ref, row_send.at[2], row_recv.at[2], {"gy": up}),
           rdma(f_ref.at[:, :DEPTH, :], fb_ref, row_send.at[3], row_recv.at[3], {"gy": up})]
    strip_down = rdma(mid_ref, top_ref, gy_send.at[0], gy_recv.at[0], {"gy": down})
    strip_up = rdma(mid_ref, bot_ref, gy_send.at[1], gy_recv.at[1], {"gy": up})

    @pl.when(has_down)
    def _():
        for c in downs:
            c.start()

    @pl.when(has_up)
    def _():
        for c in ups:
            c.start()

    pack_from(q_ref, 0)
    pack_from(f_ref, members)
    to_right = rdma(pack.at[0], mid_ref.at[0], gx_send.at[0], gx_recv.at[0], {"gx": right})
    to_left = rdma(pack.at[1], mid_ref.at[1], gx_send.at[1], gx_recv.at[1], {"gx": left})
    to_right.start()
    to_left.start()
    to_right.wait()
    to_left.wait()

    @pl.when(has_down)
    def _():
        strip_down.start()

    @pl.when(has_up)
    def _():
        strip_up.start()

    @pl.when(has_down)
    def _():
        for c in downs + [strip_down]:
            c.wait_send()
        for c in ups + [strip_up]:
            c.wait_recv()

    @pl.when(has_up)
    def _():
        for c in ups + [strip_up]:
            c.wait_send()
        for c in downs + [strip_down]:
            c.wait_recv()


def halo_exchange(mesh, state, forcing, u_vel, v_vel, land):
    members, rows, cols = state.shape
    nf = 16
    total = members + nf
    sds = jax.ShapeDtypeStruct
    return pl.pallas_call(
        functools.partial(halo_kernel, mesh.shape["gx"], mesh.shape["gy"]),
        out_shape=[sds((nf, rows, cols), F32), sds((members, DEPTH, cols), F32), sds((members, DEPTH, cols), F32),
                   sds((nf, DEPTH, cols), F32), sds((nf, DEPTH, cols), F32),
                   sds((2, total, cols), F32), sds((2, total, cols), F32), sds((2, total, cols), F32)],
        in_specs=[vspec()] * 5,
        out_specs=[vspec()] * 8,
        scratch_shapes=[VM((2, total, cols), F32)]
        + [pltpu.SemaphoreType.DMA((4,))] * 2
        + [pltpu.SemaphoreType.DMA((2,))] * 4,
        compiler_params=pltpu.CompilerParams(collective_id=0, has_side_effects=True),
        name="halo",
    )(state, forcing, u_vel, v_vel, land)


def model_kernel(n_gy, q_ref, qt_ref, qb_ref, f_ref, ft_ref, fb_ref, mid_ref, top_ref, bot_ref,
                 mode_ref, theta_ref, index_ref, out_ref, obs_ref,
                 Q, L, FO, US, H, LH, FH, UH, TH):
    gy = lax.axis_index("gy")
    members = mode_ref.shape[1]
    cols = q_ref.shape[1]
    rows = q_ref.shape[0] // members
    n_rows = rows + 2 * DEPTH
    has_up, has_down = gy > 0, gy < n_gy - 1
    shape = (8, cols)
    lane = lax.broadcasted_iota(jnp.int32, shape, 1)
    sub = lax.broadcasted_iota(jnp.int32, shape, 0)
    half_ok = jnp.where(lane < cols // 2, has_down.astype(jnp.int32), has_up.astype(jnp.int32)) > 0
    bits = {k: jnp.bitwise_and(lane, k) != 0 for k in (1, 2, 4)}

    def roll(x, k):
        return pltpu.roll(x, k % cols, 1)

    def butterfly(xs):
        xs = list(xs)
        for k in (1, 2, 4):
            for v in range(8):
                if not v & k:
                    x, y = xs[v], xs[v | k]
                    xs[v] = jnp.where(bits[k], roll(y, k), x)
                    xs[v | k] = jnp.where(bits[k], y, roll(x, -k))
        return xs

    def masked(i, x):
        if i < DEPTH:
            return jnp.where(has_up, x, 0.0)
        if i >= DEPTH + rows:
            return jnp.where(has_down, x, 0.0)
        return x

    def masked_half(half, x):
        return jnp.where(half_ok, x, 0.0) if half else x

    def gather(x, idx, axis):
        return jnp.take_along_axis(x, idx, axis=axis, mode="promise_in_bounds")

    def strip(side, half, pick):
        if half:
            x = jnp.where(lane < cols // 2, pick(bot_ref, side), pick(top_ref, side))
            return masked_half(1, x)
        return pick(mid_ref, side)

    TH[...] = jnp.zeros_like(TH)
    TH[0:theta_ref.shape[0], 0:members] = theta_ref[...]
    slot = sub * 8 + jnp.bitwise_and(lane, 7)
    par = [gather(jnp.broadcast_to(TH[k:k + 1, :], shape), slot, 1) for k in range(4)]
    diffuse = 0.05 * (1.0 + 0.5 * jnp.tanh(par[0]))
    hyper = 0.005 * (1.0 + 0.5 * jnp.tanh(par[1]))
    keep = 1.0 - 0.05 * (1.0 + 0.5 * jnp.tanh(par[2]))
    gain = par[3]
    mrow = jnp.concatenate([mode_ref[...], jnp.zeros((1, cols - members), jnp.int32)], axis=1)
    mrow = jnp.broadcast_to(mrow, shape)
    modes = [gather(mrow, sub * 8 + v, 1) for v in range(8)]

    block0 = lane - jnp.bitwise_and(lane, 7)
    for f in range(3):
        for j in range(n_rows // 8):
            if j == 0:
                x = jnp.where(has_up, ft_ref[pl.ds((8 + f) * DEPTH, 8), :], 0.0)
            elif j == n_rows // 8 - 1:
                x = jnp.where(has_down, fb_ref[pl.ds((8 + f) * DEPTH, 8), :], 0.0)
            else:
                x = f_ref[pl.ds((8 + f) * rows + (j - 1) * 8, 8), :]
            x = x if f == 2 else 0.5 * x
            for c in range(8):
                US[f, c, pl.ds(j * 8, 8), :] = gather(x, block0 + c, 1)
    scale = jnp.where(sub < 2, 0.5, 1.0)
    for side in range(2):
        for half in range(2):
            x = scale * strip(side, half, lambda ref, sd: ref[sd, members + 8:members + 16, :])
            for c in range(8):
                UH[side, c, half] = gather(x, block0 + c, 1)
            x = strip(side, half, lambda ref, sd: ref[sd, members:members + 8, :])
            ys = butterfly([gather(x, modes[v], 0) for v in range(8)])
            for c in range(8):
                FH[side, c, half] = gain * ys[c]
            ys = butterfly([strip(side, half, lambda ref, sd: ref[sd, pl.ds(v, 8, stride=8), :]) for v in range(8)])
            for c in range(8):
                H[0, side, c, half] = ys[c]

    def enter(ref, per, fr, base, ok):
        def body(k, carry):
            def keep_in(x):
                return x if ok is None else jnp.where(ok, x, 0.0)
            ys = butterfly([keep_in(ref[pl.ds(v * per + k, 8, stride=8 * per), :]) for v in range(8)])
            x = keep_in(fr[pl.ds(k, 8, stride=per), :])
            zs = butterfly([gather(x, modes[v], 0) for v in range(8)])
            for c in range(8):
                Q[0, base + k, c] = ys[c]
                FO[base + k, c] = gain * zs[c]
            return carry
        lax.fori_loop(0, per, body, 0)

    enter(qt_ref, DEPTH, ft_ref, 0, has_up)
    enter(q_ref, rows, f_ref, DEPTH, None)
    enter(qb_ref, DEPTH, fb_ref, DEPTH + rows, has_down)

    first, last = lane < 8, lane >= cols - 8

    def place(i):
        j = i - DEPTH
        return (0, j) if 0 <= j < rows else (1, (i - DEPTH - rows) % n_rows)

    def across(x, get, i):
        half, j = place(i)
        left = jnp.where(first, roll(get(0, 7, half), -8 * j), roll(x(7), 8))
        right = jnp.where(last, roll(get(1, 0, half), cols - 8 - 8 * j), roll(x(0), -8))
        return left, right

    def inward(x, lo, hi):
        left = [jnp.zeros(shape, F32)] * 2
        right = [jnp.zeros(shape, F32)] * 2
        for i in range(lo, hi):
            half, j = place(i)
            here = block0 == 8 * j
            left[half] = jnp.where(here, roll(x(i, 0), 8 * j), left[half])
            right[half] = jnp.where(here, roll(x(i, 7), 8 * j - (cols - 8)), right[half])
        return left, right

    def vertical(m, t):
        mn, tn, mp, tp = roll(m, -8), roll(t, -8), roll(m, 8), roll(t, 8)
        return ((jnp.where(last, tn, mn), jnp.where(last, mn, tn)),
                (jnp.where(first, tp, mp), jnp.where(first, mp, tp)))

    zero = jnp.zeros(shape, F32)

    def halo_x(get, ins, side, c, half):
        left, right = ins
        if c > 0:
            xm = get(side, c - 1, half)
        else:
            xm = right[half] if side == 1 else zero
        if c < 7:
            xp = get(side, c + 1, half)
        else:
            xp = left[half] if side == 0 else zero
        return xm, xp

    for s in range(STEPS):
        src, dst = s % 2, (s + 1) % 2
        lo, hi = 2 * s, n_rows - 2 * s
        final = s == STEPS - 1
        qa = lambda i, c: Q[src, i, c]
        qh = lambda side, c, half: H[src, side, c, half]
        lh = lambda side, c, half: LH[side, c, half]
        la = lambda i, c: L[i, c]
        ins = inward(qa, lo, hi)
        grads = {}
        for side in range(2):
            for c in range(8):
                m, t = qh(side, c, 0), qh(side, c, 1)
                nxt, prv = vertical(m, t)
                for half in range(2):
                    mid = (m, t)[half]
                    xm, xp = halo_x(qh, ins, side, c, half)
                    lap = (nxt[half] + prv[half]) + (xp + xm) - 4.0 * mid
                    LH[side, c, half] = masked_half(half, lap)
                    if not final:
                        grads[side, c, half] = (UH[side, c, half, 0:1] * (xp - xm)
                                                + UH[side, c, half, 1:2] * (nxt[half] - prv[half]))
        adv = {}
        def first_pass(i):
            left, right = across(lambda c: qa(i, c), qh, i)
            row = [qa(i, c) for c in range(8)]
            for c in range(8):
                xm = row[c - 1] if c else left
                xp = row[c + 1] if c < 7 else right
                up, dn = qa(i + 1, c), qa(i - 1, c)
                L[i, c] = masked(i, (up + dn) + (xp + xm) - 4.0 * row[c])
                if lo + 2 <= i < hi - 2:
                    adv[i, c] = (US[0, c, i:i + 1, :] * (xp - xm) + US[1, c, i:i + 1, :] * (up - dn))
                    adv[i, c] = keep * row[c] + (FO[i, c] - adv[i, c])

        def second_pass(i):
            left, right = across(lambda c: la(i, c), lh, i)
            row = [la(i, c) for c in range(8)]
            outs = []
            for c in range(8):
                xm = row[c - 1] if c else left
                xp = row[c + 1] if c < 7 else right
                bi = (la(i + 1, c) + la(i - 1, c)) + (xp + xm) - 4.0 * row[c]
                new = (adv.pop((i, c)) + (diffuse * row[c] - hyper * bi)) * US[2, c, i:i + 1, :]
                if final:
                    outs.append(new)
                else:
                    Q[dst, i, c] = new
            if final:
                for v, y in enumerate(butterfly(outs)):
                    out_ref[pl.ds(v * rows + i - DEPTH, 8, stride=8 * rows), :] = y

        first_pass(lo + 1)
        first_pass(lo + 2)
        for i in range(lo + 2, hi - 2):
            first_pass(i + 1)
            second_pass(i)
        if final:
            break
        ins = inward(la, lo + 1, hi - 1)
        for side in range(2):
            for c in range(8):
                m, t = lh(side, c, 0), lh(side, c, 1)
                nxt, prv = vertical(m, t)
                for half in range(2):
                    mid = (m, t)[half]
                    xm, xp = halo_x(lh, ins, side, c, half)
                    bi = (nxt[half] + prv[half]) + (xp + xm) - 4.0 * mid
                    new = (keep * qh(side, c, half) + (FH[side, c, half] - grads[side, c, half])
                           + (diffuse * mid - hyper * bi))
                    H[dst, side, c, half] = new * UH[side, c, half, 2:3]

    index = index_ref[0]
    col = jnp.bitwise_and(index, cols - 1)
    row = jnp.right_shift(index, cols.bit_length() - 1)
    hot = (lax.broadcasted_iota(jnp.int32, (cols, cols), 0) == col).astype(jnp.bfloat16)
    row_id = lax.broadcasted_iota(jnp.int32, (8, rows, cols), 1)
    dot = functools.partial(jnp.dot, preferred_element_type=F32)
    for g in range(members // 8):
        x = out_ref[pl.ds(g * 8 * rows, 8 * rows), :]
        x1 = x.astype(jnp.bfloat16)
        rem = x - x1.astype(F32)
        x2 = rem.astype(jnp.bfloat16)
        x3 = (rem - x2.astype(F32)).astype(jnp.bfloat16)
        picked = dot(x1, hot) + (dot(x2, hot) + dot(x3, hot))
        obs_ref[pl.ds(g * 8, 8), :] = jnp.sum(
            jnp.where(row_id == row[None], picked.reshape(8, rows, cols), 0.0), axis=1)


def run_model(mesh, state, fields, halos, member_mode, theta, obs_index):
    members, rows, cols = state.shape
    qt, qb, ft, fb, mid, top, bot = halos
    n_rows = rows + 2 * DEPTH
    sds = jax.ShapeDtypeStruct
    reg = (8, cols)
    out, obs = pl.pallas_call(
        functools.partial(model_kernel, mesh.shape["gy"]),
        out_shape=[sds((members * rows, cols), F32), sds((members, cols), F32)],
        in_specs=[vspec()] * 12,
        out_specs=[vspec()] * 2,
        scratch_shapes=[VM((2, n_rows, 8) + reg, F32), VM((n_rows, 8) + reg, F32), VM((n_rows, 8) + reg, F32),
                        VM((3, 8, n_rows, cols), F32),
                        VM((2, 2, 8, 2) + reg, F32), VM((2, 8, 2) + reg, F32), VM((2, 8, 2) + reg, F32),
                        VM((2, 8, 2) + reg, F32), VM(reg, F32)],
        name="model",
    )(state.reshape(members * rows, cols), qt.reshape(-1, cols), qb.reshape(-1, cols),
      fields.reshape(-1, cols), ft.reshape(-1, cols), fb.reshape(-1, cols), mid, top, bot,
      member_mode.reshape(1, members), theta.T, obs_index)
    return out.reshape(members, rows, cols), obs


def sums_kernel(n_gx, n_gy, n_ens, reduce_here, obs_ref, theta_ref, val_ref, sig_ref, full_ref, c_ref, th_ref,
                obs_all, part, rs, c_own, cs, ens_send, ens_recv, rs_send, rs_recv, cs_send, cs_recv, ag_send, ag_recv):
    gx, gy, ens = lax.axis_index("gx"), lax.axis_index("gy"), lax.axis_index("ens")
    members = obs_ref.shape[0]
    n = n_gx * n_gy
    me = gy * n_gx + gx
    peers = [lax.rem(me + o, n) for o in range(1, n)] if reduce_here else []
    where = [{"gx": lax.rem(p, n_gx), "gy": lax.div(p, n_gx)} for p in peers]
    others = [lax.rem(ens + o, n_ens) for o in range(1, n_ens)]

    barrier = pltpu.get_barrier_semaphore()
    for p in others:
        pl.semaphore_signal(barrier, inc=1, device_id={"ens": p}, device_id_type=MESH)
    for p in where:
        pl.semaphore_signal(barrier, inc=1, device_id=p, device_id_type=MESH)
    pl.semaphore_wait(barrier, len(others) + len(where))

    def rdma(src, dst, send, recv, dev):
        return pltpu.make_async_remote_copy(src_ref=src, dst_ref=dst, send_sem=send, recv_sem=recv,
                                            device_id=dev, device_id_type=MESH)

    mine = pl.ds(pl.multiple_of(ens * members, members), members)
    obs_copies, th_copies = [], []
    for k, p in enumerate(others):
        obs_copies.append(rdma(obs_ref, obs_all.at[mine], ens_send.at[2 * k], ens_recv.at[2 * k], {"ens": p}))
        th_copies.append(rdma(theta_ref, th_ref.at[ens], ens_send.at[2 * k + 1], ens_recv.at[2 * k + 1], {"ens": p}))
    for c in obs_copies + th_copies:
        c.start()
    obs_all[mine, :] = obs_ref[...]
    th_ref[ens] = theta_ref[...]
    for c in obs_copies:
        c.wait()

    x = obs_all[...]
    mean = jnp.mean(x, axis=0, keepdims=True)
    inv = 1.0 / sig_ref[0]
    anom = (x - mean) * inv
    d = jnp.broadcast_to((val_ref[0] - mean) * inv, (8, x.shape[1]))
    nt = (((1,), (1,)), ((), ()))
    total = x.shape[0]
    c_part = lax.dot_general(d, anom, nt, preferred_element_type=F32, precision=HIGH)[0:1]
    gram = lax.dot_general(anom, anom, nt, preferred_element_type=F32, precision=HIGH)

    if not reduce_here:
        full_ref[...] = gram
        c_ref[...] = c_part
        for c in th_copies:
            c.wait()
        return
    c_own[...] = c_part
    part[...] = gram
    own = total // n
    at = lambda p: pl.ds(pl.multiple_of(p * own, own), own)
    sends = [rdma(part.at[at(p)], rs.at[k], rs_send.at[k], rs_recv.at[k], w)
             for k, (p, w) in enumerate(zip(peers, where))]
    c_sends = [rdma(c_own, cs.at[k], cs_send.at[k], cs_recv.at[k], w) for k, w in enumerate(where)]
    for c in sends + c_sends:
        c.start()
    acc = part[at(me), :]
    for k, c in enumerate(sends):
        c.wait_recv()
        acc = acc + rs[k]
    full_ref[at(me), :] = acc
    gathers = [rdma(full_ref.at[at(me)], full_ref.at[at(me)], ag_send.at[k], ag_recv.at[k], w)
               for k, w in enumerate(where)]
    for c in gathers:
        c.start()
    acc = c_own[...]
    for k, c in enumerate(c_sends):
        c.wait_recv()
        acc = acc + cs[k]
    c_ref[...] = acc
    for c in sends + c_sends:
        c.wait_send()
    for c in th_copies + gathers:
        c.wait()


def ensemble_sums(mesh, obs, theta, values, sigma):
    n_gx, n_gy, n_ens = mesh.shape["gx"], mesh.shape["gy"], mesh.shape["ens"]
    members, cols = obs.shape
    total = members * n_ens
    n = n_gx * n_gy
    reduce_here = total % (8 * n) == 0
    own = total // n if reduce_here else 8
    slots = n - 1 if reduce_here else 1
    sds = jax.ShapeDtypeStruct
    full, c, th = pl.pallas_call(
        functools.partial(sums_kernel, n_gx, n_gy, n_ens, reduce_here),
        out_shape=[sds((total, total), F32), sds((1, total), F32), sds((n_ens,) + theta.shape[::-1], F32)],
        in_specs=[vspec()] * 4,
        out_specs=[vspec()] * 3,
        scratch_shapes=[VM((total, cols), F32), VM((total, total), F32), VM((slots, own, total), F32),
                        VM((1, total), F32), VM((slots, 1, total), F32)]
        + [pltpu.SemaphoreType.DMA((2 * (n_ens - 1),))] * 2
        + [pltpu.SemaphoreType.DMA((slots,))] * 6,
        compiler_params=pltpu.CompilerParams(collective_id=1, has_side_effects=True),
        name="sums",
    )(obs, theta.T, values, sigma)
    if not reduce_here:
        full, c = lax.psum((full, c), ("gx", "gy"))
    return full, c, th


def solve_kernel(members, full_ref, c_ref, th_ref, out_ref, xs):
    total = full_ref.shape[0]
    blocks = total // 8
    n_ens, params = th_ref.shape[0], th_ref.shape[1]
    shape = (8, total)
    lane = lax.broadcasted_iota(jnp.int32, shape, 1)
    sub = lax.broadcasted_iota(jnp.int32, shape, 0)
    tht = jnp.concatenate([th_ref[e] for e in range(n_ens)], axis=1)
    spread = tht - jnp.mean(tht, axis=1, keepdims=True)
    xs[...] = jnp.zeros_like(xs)
    xs[0:params, :] = spread
    cols_of = xs[...].T
    A, R = [], []
    for k in range(blocks):
        rows = slice(8 * k, 8 * k + 8)
        A.append(full_ref[rows, :] + jnp.where(lane == sub + 8 * k, float(total - 1), 0.0))
        R.append(cols_of[rows])

    def splat(x):
        return jnp.broadcast_to(x, shape)

    for k in range(blocks):
        rs_, rr = [], []
        d = {}
        for j in range(8):
            row = splat(A[k][j:j + 1])
            rs_.append(row)
            rr.append(splat(R[k][j:j + 1]))
            for i in range(j, 8):
                d[j, i] = splat(row[:, 8 * k + i:8 * k + i + 1])
        inv = []
        for j in range(8):
            inv.append(1.0 / d[j, j])
            for i in range(j + 1, 8):
                m = d[j, i] * inv[j]
                rs_[i] = rs_[i] - m * rs_[j]
                rr[i] = rr[i] - m * rr[j]
                for q in range(i, 8):
                    d[i, q] = d[i, q] - m * d[j, q]
        for i in reversed(range(8)):
            for j in range(i + 1, 8):
                rs_[i] = rs_[i] - d[i, j] * rs_[j]
                rr[i] = rr[i] - d[i, j] * rr[j]
            rs_[i] = rs_[i] * inv[i]
            rr[i] = rr[i] * inv[i]
        a, r = rs_[7], rr[7]
        for j in range(7):
            a = jnp.where(sub == j, rs_[j], a)
            r = jnp.where(sub == j, rr[j], r)
        A[k], R[k] = a, r
        for i in list(range(k + 1, blocks)) + list(range(k)):
            a, r = A[i], R[i]
            for j in range(8):
                c = splat(A[i][:, 8 * k + j:8 * k + j + 1])
                if k + 1 < blocks:
                    a = a - c * rs_[j]
                r = r - c * rr[j]
            A[i], R[i] = a, r
    for k in range(blocks):
        xs[8 * k:8 * k + 8, :] = R[k]
    x = xs[...].T[0:8]
    shift = jnp.sum(x * c_ref[...], axis=1, keepdims=True)
    new = (jnp.mean(tht, axis=1, keepdims=True) + shift[0:params]) + float(total - 1) * x[0:params]
    ens = lax.axis_index("ens")
    for e in range(n_ens):
        @pl.when(ens == e)
        def _():
            out_ref[...] = new[:, e * members:(e + 1) * members]


def solve(full, c, th, theta):
    return pl.pallas_call(
        functools.partial(solve_kernel, theta.shape[0]),
        out_shape=jax.ShapeDtypeStruct(theta.shape[::-1], F32),
        in_specs=[vspec()] * 3,
        out_specs=vspec(),
        scratch_shapes=[VM(full.shape, F32)],
        name="solve",
    )(full, c, th).T


def local(mesh, state, u_vel, v_vel, land, forcing, member_mode, theta, obs_index, obs_values, obs_sigma):
    fields, *halos = halo_exchange(mesh, state, forcing, u_vel, v_vel, land)
    final, obs = run_model(mesh, state, fields, halos, member_mode, theta, obs_index)
    full, c, th = ensemble_sums(mesh, obs, theta, obs_values, obs_sigma)
    return final, solve(full, c, th, theta)


def solution(mesh):
    placed = (
        P("ens", "gy", "gx"),
        P("gy", "gx"),
        P("gy", "gx"),
        P("gy", "gx"),
        P(None, "gy", "gx"),
        P("ens"),
        P("ens", None),
        P("gy", "gx", None),
        P("gy", "gx", None),
        P("gy", "gx", None),
    )
    return jax.shard_map(
        functools.partial(local, mesh),
        mesh=mesh,
        in_specs=placed,
        out_specs=(P("ens", "gy", "gx"), P("ens", None)),
        check_vma=False,
    )
```

profile of v0, /device:TPU:0, one launch (start us, length us, event | category | flops | bytes accessed | tf_op | source)
XLA Modules:
  0.0 55.5 jit_solution(6070237614134999758)
XLA Ops:
  0.6 12.3 %halo.1 = (f32[16,16,128]{2,1,0:T(8,128)}, f32[64,8,128]{2,1,0:T(8,128)}, f32[64,8,128]{2,1,0:T(8,128)}, f32[16,8,128]{2,1,0:T(8,128)}, f32[16,8,128]{2,1,0:T(8,...) custom-call(f32[64,16,128]{2,1,0:T(8,128)} %q_ref.1, f32[8,16,128]{2,1,0:T(8,128)} %forcing_ref.1, ...), custom_call_target="tpu_custom_call" | custom-call | tf_op jit(solution)/shard_map/halo/pallas_call | solution.py:125
  12.9 16.1 %model.1 = (f32[1024,128]{1,0:T(8,128)}, f32[64,128]{1,0:T(8,128)}) custom-call(f32[1024,128]{1,0:T(8,128)} %bitcast.10, f32[512,128]{1,0:T(8,128)} %bitcast.11, f32[512,128]{1,0:T(8,128)} %bitcast.12, f32[256,128]{1,0:T(8,128)} %bitcast.13, f32[128,128]{1,0:T(8,128)} %bitcast.14, f32[128,128]{1,0:T(8,128)} %bitcast.15, ...), custom_call_target="tpu_custom_call" | custom-call | tf_op jit(solution)/shard_map/model/pallas_call | solution.py:378
  29.0 20.3 %sums.1 = (f32[128,128]{1,0:T(8,128)}, f32[1,128]{1,0:T(1,128)}, f32[2,4,64]{2,1,0:T(4,128)}) custom-call(f32[64,128]{1,0:T(8,128)} %get-tuple-element.24.obs_ref, f32[4,64]{1,0:T(4,128)} %bitcast.17, f32[1,1,128]{2,1,0:T(1,128)} %val_ref.1, f32[1,1,128]{2,1,0:T(1,128)} %sig_ref.1), custom_call_target="tpu_custom_call" | custom-call | tf_op jit(solution)/shard_map/sums/pallas_call | solution.py:481
  49.3 6.2 %solve.1 = f32[4,64]{1,0:T(4,128)} custom-call(f32[128,128]{1,0:T(8,128)} %get-tuple-element.25.full_ref, f32[1,128]{1,0:T(1,128)} %get-tuple-element.26.c_ref, f32[2,4,64]{2,1,0:T(4,128)} %get-tuple-element.27.th_ref), custom_call_target="tpu_custom_call" | custom-call | tf_op jit(solution)/shard_map/solve/pallas_call | solution.py:569
where the time goes:
time: 55.8 us; the launch traced here: 55.5 us
  Pallas kernels  54.9 us (98%)
  between operations  0.65 us (1%)
    pallas_call x1, Pallas kernels, ensemble_sums(): pl.pallas_call(functools.partial(sums_kernel, n_gx, n_gy, n_ens, reduce_h...  20.3 us
    pallas_call x1, Pallas kernels, run_model(): pl.pallas_call(functools.partial(model_kernel, mesh.shape['gy']), out_sha...  16.1 us
    pallas_call x1, Pallas kernels, halo_exchange(): pl.pallas_call(functools.partial(halo_kernel, mesh.shape['gx'], mesh.shap...  12.3 us
    pallas_call x1, Pallas kernels, solve(): pl.pallas_call(functools.partial(solve_kernel, theta.shape[0]), out_shape...  6.18 us

commit v1 on v0

v1 whole, which is shorter than its diff:
```python
import functools
import jax
import jax.numpy as jnp
from jax import lax
from jax.experimental import pallas as pl
from jax.experimental.pallas import tpu as pltpu
from jax.sharding import PartitionSpec as P

STEPS = 4
DEPTH = 2 * STEPS
F32 = jnp.float32
I32 = jnp.int32
VM = pltpu.VMEM
MESH = pl.DeviceIdType.MESH
HIGH = lax.Precision.HIGHEST


def vspec():
    return pl.BlockSpec(memory_space=pltpu.VMEM)


def anyspec():
    return pl.BlockSpec(memory_space=pl.ANY)


def flat(ref):
    return ref.reshape(ref.shape[0] * ref.shape[1], ref.shape[2])


def rdma(src, dst, send, recv, dev):
    return pltpu.make_async_remote_copy(src_ref=src, dst_ref=dst, send_sem=send, recv_sem=recv,
                                        device_id=dev, device_id_type=MESH)


def step_kernel(n_gx, n_gy, n_ens, reduce_here,
                state_ref, forcing_ref, u_ref, v_ref, land_ref, mode_in, theta_in, index_in, val_in, sig_in,
                final_ref, full_ref, c_ref, th_ref,
                q_lo, q_hi, f_lo, f_hi, land_b, mode_ref, theta_ref, index_ref, val_ref, sig_ref,
                qt_ref, qb_ref, ft_ref, fb_ref, pack, mid_ref, top_ref, bot_ref,
                Q, L, FO, US, H, LH, FH, UH, TH, out_ref,
                obs_ref, obs_all, part, rs, c_own, cs,
                load_sem, store_sem, row_send, row_recv, gx_send, gx_recv, gy_send, gy_recv,
                ens_send, ens_recv, rs_send, rs_recv, cs_send, cs_recv, ag_send, ag_recv):
    gx, gy, ens = lax.axis_index("gx"), lax.axis_index("gy"), lax.axis_index("ens")
    right, left = lax.rem(gx + 1, n_gx), lax.rem(gx + n_gx - 1, n_gx)
    has_up, has_down = gy > 0, gy < n_gy - 1
    up, down = jnp.maximum(gy - 1, 0), jnp.minimum(gy + 1, n_gy - 1)
    members, rows, cols = state_ref.shape
    patterns = forcing_ref.shape[0]
    fields = patterns + 3
    n_rows = rows + 2 * DEPTH
    n = n_gx * n_gy
    me = gy * n_gx + gx
    peers = [lax.rem(me + o, n) for o in range(1, n)] if reduce_here else []
    where = [{"gx": lax.rem(p, n_gx), "gy": lax.div(p, n_gx)} for p in peers]
    others = [lax.rem(ens + o, n_ens) for o in range(1, n_ens)]

    barrier = pltpu.get_barrier_semaphore()
    for p in others:
        pl.semaphore_signal(barrier, inc=1, device_id={"ens": p}, device_id_type=MESH)
    if reduce_here:
        for p in where:
            pl.semaphore_signal(barrier, inc=1, device_id=p, device_id_type=MESH)
        expected = len(others) + len(where)
    else:
        pl.semaphore_signal(barrier, inc=1, device_id={"gx": right}, device_id_type=MESH)
        pl.semaphore_signal(barrier, inc=1, device_id={"gx": left}, device_id_type=MESH)

        @pl.when(has_up)
        def _():
            pl.semaphore_signal(barrier, inc=1, device_id={"gy": up}, device_id_type=MESH)

        @pl.when(has_down)
        def _():
            pl.semaphore_signal(barrier, inc=1, device_id={"gy": down}, device_id_type=MESH)
        expected = len(others) + 2 + has_up.astype(I32) + has_down.astype(I32)

    pairs = [(state_ref.at[:, 0:DEPTH, :], q_lo), (state_ref.at[:, rows - DEPTH:, :], q_hi)]
    for h, dst in ((0, f_lo), (rows - DEPTH, f_hi)):
        pairs += [(forcing_ref.at[:, h:h + DEPTH, :], dst.at[0:patterns]),
                  (u_ref.at[h:h + DEPTH, :], dst.at[patterns]), (v_ref.at[h:h + DEPTH, :], dst.at[patterns + 1])]
    pairs += [(land_ref, land_b), (mode_in, mode_ref), (theta_in, theta_ref), (index_in, index_ref),
              (val_in, val_ref), (sig_in, sig_ref)]
    loads = [pltpu.make_async_copy(s, d, load_sem.at[k]) for k, (s, d) in enumerate(pairs)]
    for c in loads:
        c.start()

    shape = (8, cols)
    lane = lax.broadcasted_iota(I32, shape, 1)
    sub = lax.broadcasted_iota(I32, shape, 0)
    half_ok = jnp.where(lane < cols // 2, has_down.astype(I32), has_up.astype(I32)) > 0
    bits = {k: jnp.bitwise_and(lane, k) != 0 for k in (1, 2, 4)}

    def roll(x, k):
        return pltpu.roll(x, k % cols, 1)

    def butterfly(xs):
        xs = list(xs)
        for k in (1, 2, 4):
            for v in range(8):
                if not v & k:
                    x, y = xs[v], xs[v | k]
                    xs[v] = jnp.where(bits[k], roll(y, k), x)
                    xs[v | k] = jnp.where(bits[k], y, roll(x, -k))
        return xs

    def gather(x, idx, axis):
        return jnp.take_along_axis(x, idx, axis=axis, mode="promise_in_bounds")

    for c in loads:
        c.wait()
    for h, dst in ((0, f_lo), (rows - DEPTH, f_hi)):
        dst[patterns + 2] = (1 - land_b[h:h + DEPTH, :]).astype(F32)
        dst[fields:] = jnp.zeros((dst.shape[0] - fields, DEPTH, cols), F32)

    pl.semaphore_wait(barrier, expected)

    downs = [rdma(q_hi, qt_ref, row_send.at[0], row_recv.at[0], {"gy": down}),
             rdma(f_hi.at[0:fields], ft_ref.at[0:fields], row_send.at[1], row_recv.at[1], {"gy": down})]
    ups = [rdma(q_lo, qb_ref, row_send.at[2], row_recv.at[2], {"gy": up}),
           rdma(f_lo.at[0:fields], fb_ref.at[0:fields], row_send.at[3], row_recv.at[3], {"gy": up})]
    strip_down = rdma(mid_ref, top_ref, gy_send.at[0], gy_recv.at[0], {"gy": down})
    strip_up = rdma(mid_ref, bot_ref, gy_send.at[1], gy_recv.at[1], {"gy": up})

    @pl.when(has_down)
    def _():
        for c in downs:
            c.start()

    @pl.when(has_up)
    def _():
        for c in ups:
            c.start()

    def pack_from(lo_ref, hi_ref, base):
        for g in range(lo_ref.shape[0] // 8):
            lo = jnp.zeros(shape, F32)
            hi = jnp.zeros(shape, F32)
            for r in range(rows):
                ref = flat(lo_ref if r < DEPTH else hi_ref)
                val = ref[pl.ds(g * 8 * DEPTH + r % DEPTH, 8, stride=DEPTH), :]
                mine = (lane // DEPTH) == r
                hi = jnp.where(mine, roll(val, r * DEPTH + DEPTH), hi)
                lo = jnp.where(mine, roll(val, r * DEPTH), lo)
            pack[0, base + g * 8:base + g * 8 + 8, :] = hi
            pack[1, base + g * 8:base + g * 8 + 8, :] = lo

    pack_from(q_lo, q_hi, 0)
    pack_from(f_lo, f_hi, members)
    to_right = rdma(pack.at[0], mid_ref.at[0], gx_send.at[0], gx_recv.at[0], {"gx": right})
    to_left = rdma(pack.at[1], mid_ref.at[1], gx_send.at[1], gx_recv.at[1], {"gx": left})
    to_right.start()
    to_left.start()

    TH[...] = jnp.zeros_like(TH)
    TH[0:theta_ref.shape[0], 0:members] = theta_ref[...]
    slot = sub * 8 + jnp.bitwise_and(lane, 7)
    par = [gather(jnp.broadcast_to(TH[k:k + 1, :], shape), slot, 1) for k in range(4)]
    diffuse = 0.05 * (1.0 + 0.5 * jnp.tanh(par[0]))
    hyper = 0.005 * (1.0 + 0.5 * jnp.tanh(par[1]))
    keep = 1.0 - 0.05 * (1.0 + 0.5 * jnp.tanh(par[2]))
    gain = par[3]
    mrow = jnp.concatenate([mode_ref[...], jnp.zeros((1, cols - members), I32)], axis=1)
    pattern_of = gather(jnp.broadcast_to(mrow, shape), slot, 1)
    block0 = lane - jnp.bitwise_and(lane, 7)

    def spread(x):
        return [gather(x, block0 + c, 1) for c in range(8)]

    def forced(x):
        return [gain * gather(y, pattern_of, 0) for y in spread(x)]

    def enter(ref, fr, base, ok):
        ref, fr = flat(ref), flat(fr)

        def keep_in(x):
            return x if ok is None else jnp.where(ok, x, 0.0)

        for k in range(DEPTH):
            ys = butterfly([keep_in(ref[pl.ds(v * DEPTH + k, 8, stride=8 * DEPTH), :]) for v in range(8)])
            zs = forced(keep_in(fr[pl.ds(k, 8, stride=DEPTH), :]))
            for c in range(8):
                Q[0, base + k, c] = ys[c]
                FO[base + k, c] = zs[c]
        for f in range(3):
            x = keep_in(fr[(patterns + f) * DEPTH:(patterns + f + 1) * DEPTH, :])
            x = x if f == 2 else 0.5 * x
            for c, y in enumerate(spread(x)):
                US[f, c, base:base + DEPTH, :] = y

    enter(q_lo, f_lo, DEPTH, None)
    enter(q_hi, f_hi, DEPTH + rows - DEPTH, None)

    to_right.wait()
    to_left.wait()

    @pl.when(has_down)
    def _():
        strip_down.start()

    @pl.when(has_up)
    def _():
        strip_up.start()

    def masked_half(half, x):
        return jnp.where(half_ok, x, 0.0) if half else x

    def strip(side, half, pick):
        if half:
            x = jnp.where(lane < cols // 2, pick(bot_ref, side), pick(top_ref, side))
            return masked_half(1, x)
        return pick(mid_ref, side)

    scale = jnp.where(sub < 2, 0.5, 1.0)

    def enter_strip(half):
        for side in range(2):
            x = scale * strip(side, half, lambda ref, sd: ref[sd, members + patterns:members + patterns + 8, :])
            for c, y in enumerate(spread(x)):
                UH[side, c, half] = y
            for c, y in enumerate(forced(strip(side, half, lambda ref, sd: ref[sd, members:members + patterns, :]))):
                FH[side, c, half] = y
            ys = butterfly([strip(side, half, lambda ref, sd: ref[sd, pl.ds(v, 8, stride=8), :]) for v in range(8)])
            for c in range(8):
                H[0, side, c, half] = ys[c]

    enter_strip(0)

    @pl.when(has_down)
    def _():
        for c in ups:
            c.wait_recv()
        strip_up_recv = rdma(mid_ref, bot_ref, gy_send.at[1], gy_recv.at[1], {"gy": up})
        strip_up_recv.wait_recv()

    @pl.when(has_up)
    def _():
        for c in downs:
            c.wait_recv()
        strip_down.wait_recv()

    enter(qt_ref, ft_ref, 0, has_up)
    enter(qb_ref, fb_ref, DEPTH + rows, has_down)
    enter_strip(1)

    def masked(i, x):
        if i < DEPTH:
            return jnp.where(has_up, x, 0.0)
        if i >= DEPTH + rows:
            return jnp.where(has_down, x, 0.0)
        return x

    first, last = lane < 8, lane >= cols - 8

    def place(i):
        j = i - DEPTH
        return (0, j) if 0 <= j < rows else (1, (i - DEPTH - rows) % n_rows)

    def across(x, get, i):
        half, j = place(i)
        left = jnp.where(first, roll(get(0, 7, half), -8 * j), roll(x(7), 8))
        right = jnp.where(last, roll(get(1, 0, half), cols - 8 - 8 * j), roll(x(0), -8))
        return left, right

    def inward(x, lo, hi):
        left = [jnp.zeros(shape, F32)] * 2
        right = [jnp.zeros(shape, F32)] * 2
        for i in range(lo, hi):
            half, j = place(i)
            here = block0 == 8 * j
            left[half] = jnp.where(here, roll(x(i, 0), 8 * j), left[half])
            right[half] = jnp.where(here, roll(x(i, 7), 8 * j - (cols - 8)), right[half])
        return left, right

    def vertical(m, t):
        mn, tn, mp, tp = roll(m, -8), roll(t, -8), roll(m, 8), roll(t, 8)
        return ((jnp.where(last, tn, mn), jnp.where(last, mn, tn)),
                (jnp.where(first, tp, mp), jnp.where(first, mp, tp)))

    zero = jnp.zeros(shape, F32)

    def halo_x(get, ins, side, c, half):
        left, right = ins
        if c > 0:
            xm = get(side, c - 1, half)
        else:
            xm = right[half] if side == 1 else zero
        if c < 7:
            xp = get(side, c + 1, half)
        else:
            xp = left[half] if side == 0 else zero
        return xm, xp

    for s in range(STEPS):
        src, dst = s % 2, (s + 1) % 2
        lo, hi = 2 * s, n_rows - 2 * s
        final = s == STEPS - 1
        qa = lambda i, c: Q[src, i, c]
        qh = lambda side, c, half: H[src, side, c, half]
        lh = lambda side, c, half: LH[side, c, half]
        la = lambda i, c: L[i, c]
        ins = inward(qa, lo, hi)
        grads = {}
        for side in range(2):
            for c in range(8):
                m, t = qh(side, c, 0), qh(side, c, 1)
                nxt, prv = vertical(m, t)
                for half in range(2):
                    mid = (m, t)[half]
                    xm, xp = halo_x(qh, ins, side, c, half)
                    lap = (nxt[half] + prv[half]) + (xp + xm) - 4.0 * mid
                    LH[side, c, half] = masked_half(half, lap)
                    if not final:
                        grads[side, c, half] = (UH[side, c, half, 0:1] * (xp - xm)
                                                + UH[side, c, half, 1:2] * (nxt[half] - prv[half]))
        adv = {}
        def first_pass(i):
            left, right = across(lambda c: qa(i, c), qh, i)
            row = [qa(i, c) for c in range(8)]
            for c in range(8):
                xm = row[c - 1] if c else left
                xp = row[c + 1] if c < 7 else right
                up_, dn = qa(i + 1, c), qa(i - 1, c)
                L[i, c] = masked(i, (up_ + dn) + (xp + xm) - 4.0 * row[c])
                if lo + 2 <= i < hi - 2:
                    adv[i, c] = (US[0, c, i:i + 1, :] * (xp - xm) + US[1, c, i:i + 1, :] * (up_ - dn))
                    adv[i, c] = keep * row[c] + (FO[i, c] - adv[i, c])

        def second_pass(i):
            left, right = across(lambda c: la(i, c), lh, i)
            row = [la(i, c) for c in range(8)]
            outs = []
            for c in range(8):
                xm = row[c - 1] if c else left
                xp = row[c + 1] if c < 7 else right
                bi = (la(i + 1, c) + la(i - 1, c)) + (xp + xm) - 4.0 * row[c]
                new = (adv.pop((i, c)) + (diffuse * row[c] - hyper * bi)) * US[2, c, i:i + 1, :]
                if final:
                    outs.append(new)
                else:
                    Q[dst, i, c] = new
            if final:
                for v, y in enumerate(butterfly(outs)):
                    out_ref[pl.ds(v * rows + i - DEPTH, 8, stride=8 * rows), :] = y

        first_pass(lo + 1)
        first_pass(lo + 2)
        for i in range(lo + 2, hi - 2):
            first_pass(i + 1)
            second_pass(i)
        if final:
            break
        ins = inward(la, lo + 1, hi - 1)
        for side in range(2):
            for c in range(8):
                m, t = lh(side, c, 0), lh(side, c, 1)
                nxt, prv = vertical(m, t)
                for half in range(2):
                    mid = (m, t)[half]
                    xm, xp = halo_x(lh, ins, side, c, half)
                    bi = (nxt[half] + prv[half]) + (xp + xm) - 4.0 * mid
                    new = (keep * qh(side, c, half) + (FH[side, c, half] - grads[side, c, half])
                           + (diffuse * mid - hyper * bi))
                    H[dst, side, c, half] = new * UH[side, c, half, 2:3]

    index = index_ref[0]
    col = jnp.bitwise_and(index, cols - 1)
    row = jnp.right_shift(index, cols.bit_length() - 1)
    hot = (lax.broadcasted_iota(I32, (cols, cols), 0) == col).astype(jnp.bfloat16)
    row_id = lax.broadcasted_iota(I32, (8, rows, cols), 1)
    dot = functools.partial(jnp.dot, preferred_element_type=F32)
    for g in range(members // 8):
        x = out_ref[pl.ds(g * 8 * rows, 8 * rows), :]
        x1 = x.astype(jnp.bfloat16)
        rem = x - x1.astype(F32)
        x2 = rem.astype(jnp.bfloat16)
        x3 = (rem - x2.astype(F32)).astype(jnp.bfloat16)
        picked = dot(x1, hot) + (dot(x2, hot) + dot(x3, hot))
        obs_ref[pl.ds(g * 8, 8), :] = jnp.sum(
            jnp.where(row_id == row[None], picked.reshape(8, rows, cols), 0.0), axis=1)

    mine = pl.ds(pl.multiple_of(ens * members, members), members)
    obs_copies, th_copies = [], []
    for k, p in enumerate(others):
        obs_copies.append(rdma(obs_ref, obs_all.at[mine], ens_send.at[2 * k], ens_recv.at[2 * k], {"ens": p}))
        th_copies.append(rdma(theta_ref, th_ref.at[ens], ens_send.at[2 * k + 1], ens_recv.at[2 * k + 1], {"ens": p}))
    for c in obs_copies + th_copies:
        c.start()
    store = pltpu.make_async_copy(out_ref, final_ref, store_sem.at[0])
    store.start()
    obs_all[mine, :] = obs_ref[...]
    th_ref[ens] = theta_ref[...]
    for c in obs_copies:
        c.wait()

    x = obs_all[...]
    mean = jnp.mean(x, axis=0, keepdims=True)
    inv = 1.0 / sig_ref[0]
    anom = (x - mean) * inv
    d = jnp.broadcast_to((val_ref[0] - mean) * inv, (8, x.shape[1]))
    nt = (((1,), (1,)), ((), ()))
    total = x.shape[0]
    c_part = lax.dot_general(d, anom, nt, preferred_element_type=F32, precision=HIGH)[0:1]
    gram = lax.dot_general(anom, anom, nt, preferred_element_type=F32, precision=HIGH)

    def finish():
        to_send = [(has_down, downs + [strip_down]), (has_up, ups + [strip_up])]
        for ok, copies in to_send:
            @pl.when(ok)
            def _():
                for c in copies:
                    c.wait_send()
        for c in th_copies:
            c.wait()
        store.wait()

    if not reduce_here:
        full_ref[...] = gram
        c_ref[...] = c_part
        finish()
        return
    c_own[...] = c_part
    part[...] = gram
    own = total // n
    at = lambda p: pl.ds(pl.multiple_of(p * own, own), own)
    sends = [rdma(part.at[at(p)], rs.at[k], rs_send.at[k], rs_recv.at[k], w)
             for k, (p, w) in enumerate(zip(peers, where))]
    c_sends = [rdma(c_own, cs.at[k], cs_send.at[k], cs_recv.at[k], w) for k, w in enumerate(where)]
    for c in sends + c_sends:
        c.start()
    acc = part[at(me), :]
    for k, c in enumerate(sends):
        c.wait_recv()
        acc = acc + rs[k]
    full_ref[at(me), :] = acc
    gathers = [rdma(full_ref.at[at(me)], full_ref.at[at(me)], ag_send.at[k], ag_recv.at[k], w)
               for k, w in enumerate(where)]
    for c in gathers:
        c.start()
    acc = c_own[...]
    for k, c in enumerate(c_sends):
        c.wait_recv()
        acc = acc + cs[k]
    c_ref[...] = acc
    for c in sends + c_sends:
        c.wait_send()
    finish()
    for c in gathers:
        c.wait()


def run_step(mesh, state, forcing, u_vel, v_vel, land, member_mode, theta, obs_index, values, sigma):
    n_gx, n_gy, n_ens = mesh.shape["gx"], mesh.shape["gy"], mesh.shape["ens"]
    members, rows, cols = state.shape
    patterns = forcing.shape[0]
    sites = obs_index.shape[-1]
    params = theta.shape[1]
    nf = -(-(patterns + 3) // 8) * 8
    strips = members + nf
    n_rows = rows + 2 * DEPTH
    total = members * n_ens
    n = n_gx * n_gy
    reduce_here = total % (8 * n) == 0
    own = total // n if reduce_here else 8
    slots = n - 1 if reduce_here else 1
    sds = jax.ShapeDtypeStruct
    dma = pltpu.SemaphoreType.DMA
    reg = (8, cols)
    final, full, c, th = pl.pallas_call(
        functools.partial(step_kernel, n_gx, n_gy, n_ens, reduce_here),
        out_shape=[sds((members * rows, cols), F32), sds((total, total), F32), sds((1, total), F32),
                   sds((n_ens, params, members), F32)],
        in_specs=[anyspec()] * 10,
        out_specs=[anyspec()] + [vspec()] * 3,
        scratch_shapes=[VM((members, DEPTH, cols), F32)] * 2 + [VM((nf, DEPTH, cols), F32)] * 2
        + [VM((rows, cols), I32), VM((1, members), I32), VM((params, members), F32), VM((1, 1, sites), I32),
           VM((1, 1, sites), F32), VM((1, 1, sites), F32)]
        + [VM((members, DEPTH, cols), F32)] * 2 + [VM((nf, DEPTH, cols), F32)] * 2
        + [VM((2, strips, cols), F32)] * 4
        + [VM((2, n_rows, 8) + reg, F32), VM((n_rows, 8) + reg, F32), VM((n_rows, 8) + reg, F32),
           VM((3, 8, n_rows, cols), F32),
           VM((2, 2, 8, 2) + reg, F32), VM((2, 8, 2) + reg, F32), VM((2, 8, 2) + reg, F32),
           VM((2, 8, 2) + reg, F32), VM(reg, F32), VM((members * rows, cols), F32)]
        + [VM((members, sites), F32), VM((total, sites), F32), VM((total, total), F32), VM((slots, own, total), F32),
           VM((1, total), F32), VM((slots, 1, total), F32)]
        + [dma((14,)), dma((1,)), dma((4,)), dma((4,)), dma((2,)), dma((2,)), dma((2,)), dma((2,))]
        + [dma((2 * (n_ens - 1),))] * 2 + [dma((slots,))] * 6,
        compiler_params=pltpu.CompilerParams(collective_id=0, has_side_effects=True),
        name="step",
    )(state, forcing, u_vel, v_vel, land, member_mode.reshape(1, members), theta.T, obs_index, values, sigma)
    if not reduce_here:
        full, c = lax.psum((full, c), ("gx", "gy"))
    return final, full, c, th


def solve_kernel(members, full_ref, c_ref, th_ref, out_ref, xs):
    total = full_ref.shape[0]
    blocks = total // 8
    n_ens, params = th_ref.shape[0], th_ref.shape[1]
    shape = (8, total)
    lane = lax.broadcasted_iota(jnp.int32, shape, 1)
    sub = lax.broadcasted_iota(jnp.int32, shape, 0)
    tht = jnp.concatenate([th_ref[e] for e in range(n_ens)], axis=1)
    spread = tht - jnp.mean(tht, axis=1, keepdims=True)
    xs[...] = jnp.zeros_like(xs)
    xs[0:params, :] = spread
    cols_of = xs[...].T
    A, R = [], []
    for k in range(blocks):
        rows = slice(8 * k, 8 * k + 8)
        A.append(full_ref[rows, :] + jnp.where(lane == sub + 8 * k, float(total - 1), 0.0))
        R.append(cols_of[rows])

    def splat(x):
        return jnp.broadcast_to(x, shape)

    for k in range(blocks):
        rs_, rr = [], []
        d = {}
        for j in range(8):
            row = splat(A[k][j:j + 1])
            rs_.append(row)
            rr.append(splat(R[k][j:j + 1]))
            for i in range(j, 8):
                d[j, i] = splat(row[:, 8 * k + i:8 * k + i + 1])
        inv = []
        for j in range(8):
            inv.append(1.0 / d[j, j])
            for i in range(j + 1, 8):
                m = d[j, i] * inv[j]
                rs_[i] = rs_[i] - m * rs_[j]
                rr[i] = rr[i] - m * rr[j]
                for q in range(i, 8):
                    d[i, q] = d[i, q] - m * d[j, q]
        for i in reversed(range(8)):
            for j in range(i + 1, 8):
                rs_[i] = rs_[i] - d[i, j] * rs_[j]
                rr[i] = rr[i] - d[i, j] * rr[j]
            rs_[i] = rs_[i] * inv[i]
            rr[i] = rr[i] * inv[i]
        a, r = rs_[7], rr[7]
        for j in range(7):
            a = jnp.where(sub == j, rs_[j], a)
            r = jnp.where(sub == j, rr[j], r)
        A[k], R[k] = a, r
        for i in list(range(k + 1, blocks)) + list(range(k)):
            a, r = A[i], R[i]
            for j in range(8):
                c = splat(A[i][:, 8 * k + j:8 * k + j + 1])
                if k + 1 < blocks:
                    a = a - c * rs_[j]
                r = r - c * rr[j]
            A[i], R[i] = a, r
    for k in range(blocks):
        xs[8 * k:8 * k + 8, :] = R[k]
    x = xs[...].T[0:8]
    shift = jnp.sum(x * c_ref[...], axis=1, keepdims=True)
    new = (jnp.mean(tht, axis=1, keepdims=True) + shift[0:params]) + float(total - 1) * x[0:params]
    ens = lax.axis_index("ens")
    for e in range(n_ens):
        @pl.when(ens == e)
        def _():
            out_ref[...] = new[:, e * members:(e + 1) * members]


def relay_kernel(members, full_ref, c_ref, th_ref, raw_ref, out_ref, final_ref, xs, buf, sem):
    take = pltpu.make_async_copy(raw_ref, buf, sem.at[0])
    take.start()
    take.wait()
    give = pltpu.make_async_copy(buf, final_ref, sem.at[1])
    give.start()
    solve_kernel(members, full_ref, c_ref, th_ref, out_ref, xs)
    give.wait()


def solve(full, c, th, theta, raw):
    out, final = pl.pallas_call(
        functools.partial(relay_kernel, theta.shape[0]),
        out_shape=[jax.ShapeDtypeStruct(theta.shape[::-1], F32), jax.ShapeDtypeStruct(raw.shape, F32)],
        in_specs=[vspec()] * 3 + [anyspec()],
        out_specs=[vspec(), anyspec()],
        scratch_shapes=[VM(full.shape, F32), VM(raw.shape, F32), pltpu.SemaphoreType.DMA((2,))],
        name="solve",
    )(full, c, th, raw)
    return out.T, final


def local(mesh, state, u_vel, v_vel, land, forcing, member_mode, theta, obs_index, obs_values, obs_sigma):
    raw, full, c, th = run_step(mesh, state, forcing, u_vel, v_vel, land, member_mode, theta, obs_index,
                                obs_values, obs_sigma)
    new_theta, final = solve(full, c, th, theta, raw)
    return final.reshape(state.shape), new_theta


def solution(mesh):
    placed = (
        P("ens", "gy", "gx"),
        P("gy", "gx"),
        P("gy", "gx"),
        P("gy", "gx"),
        P(None, "gy", "gx"),
        P("ens"),
        P("ens", None),
        P("gy", "gx", None),
        P("gy", "gx", None),
        P("gy", "gx", None),
    )
    return jax.shard_map(
        functools.partial(local, mesh),
        mesh=mesh,
        in_specs=placed,
        out_specs=(P("ens", "gy", "gx"), P("ens", None)),
        check_vma=False,
    )
```

time: 55.8 us -> 42.5 us (0.76)
  Pallas kernels: 54.9 us -> 41.6 us
    pallas_call x4 -> x2, Pallas kernels: 54.9 us -> 41.6 us  [the longest x1 34.4 us: run_step(): pl.pallas_call(functools.partial(step_kernel, n_gx, n_gy, n_ens, reduce_h...]
where the time goes in v1:
time: 42.5 us; the launch traced here: 42.3 us
  Pallas kernels  41.6 us (98%)
  between operations  0.64 us (2%)
    pallas_call x1, Pallas kernels, run_step(): pl.pallas_call(functools.partial(step_kernel, n_gx, n_gy, n_ens, reduce_h...  34.4 us
    pallas_call x1, Pallas kernels, solve(): pl.pallas_call(functools.partial(relay_kernel, theta.shape[0]), out_shape...  7.24 us

profile of v1, /device:TPU:0, one launch (start us, length us, event | category | flops | bytes accessed | tf_op | source)
XLA Modules:
  0.0 42.3 jit_solution(12923459182705746549)
XLA Ops:
  0.6 34.4 %step.1 = (f32[1024,128]{1,0:T(8,128)}, f32[128,128]{1,0:T(8,128)}, f32[1,128]{1,0:T(1,128)}, f32[2,4,64]{2,1,0:T(4,128)}) custom-call(f32[64,16,128]{2,1,0:T(8,128)} %state_ref.1, f32[8,16,128]{2,1,0:T(8,128)} %forcing_ref.1, f32[16,128]{1,0:T(8,128)} %u_ref.1, f32[16,128]{1,0:T(8,128)} %v_ref.1, s32[16,128]{1,0:T(8,128)} %land_ref.1, s32[1,64]{1,0:T(1,128)} %bitcast.5, ...), custom_call_target="tpu_custom_call" | custom-call | tf_op jit(solution)/shard_map/step/pallas_call | solution.py:469
  35.0 7.2 %solve.1 = (f32[4,64]{1,0:T(4,128)}, f32[1024,128]{1,0:T(8,128)}) custom-call(f32[128,128]{1,0:T(8,128)} %get-tuple-element.8.full_ref, f32[1,128]{1,0:T(1,128)} %get-tuple-element.9.c_ref, f32[2,4,64]{2,1,0:T(4,128)} %get-tuple-element.10.th_ref, f32[1024,128]{1,0:T(8,128)} %get-tuple-element.11.raw_ref), custom_call_target="tpu_custom_call" | custom-call | tf_op jit(solution)/shard_map/solve/pallas_call | solution.py:577

commit v2 on v1

v2 whole, which is shorter than its diff:
```python
import functools
import jax
import jax.numpy as jnp
from jax import lax
from jax.experimental import pallas as pl
from jax.experimental.pallas import tpu as pltpu
from jax.sharding import PartitionSpec as P

STEPS = 4
SPACE = 24 * 2**20
SMALL_SPACE = 12 * 2**20
DEPTH = 2 * STEPS
F32 = jnp.float32
I32 = jnp.int32
VM = pltpu.VMEM
MESH = pl.DeviceIdType.MESH
HIGH = lax.Precision.HIGHEST


def vspec():
    return pl.BlockSpec(memory_space=pltpu.VMEM)


def anyspec():
    return pl.BlockSpec(memory_space=pl.ANY)


def hspec():
    return pl.BlockSpec(memory_space=pltpu.HBM)


def flat(ref):
    return ref.reshape(ref.shape[0] * ref.shape[1], ref.shape[2])


def rdma(src, dst, send, recv, dev):
    return pltpu.make_async_remote_copy(src_ref=src, dst_ref=dst, send_sem=send, recv_sem=recv,
                                        device_id=dev, device_id_type=MESH)


def step_kernel(n_gx, n_gy, n_ens, reduce_here, owners,
                state_ref, forcing_ref, u_ref, v_ref, land_ref, mode_in, theta_in, index_in, val_in, sig_in,
                out_lo, out_hi, full_ref, th_ref,
                q_lo, q_hi, f_lo, f_hi, land_b, mode_ref, theta_ref, index_ref, val_ref, sig_ref,
                qt_ref, qb_ref, ft_ref, fb_ref, pack, corner, mid_ref, top_ref, bot_ref,
                Q, L, FO, US, H, LH, FH, UH, TH,
                obs_ref, obs_all, part, rs,
                load_sem, row_send, row_recv, gx_send, gx_recv, diag_send, diag_recv,
                ens_send, ens_recv, rs_send, rs_recv, ag_send, ag_recv):
    gx, gy, ens = lax.axis_index("gx"), lax.axis_index("gy"), lax.axis_index("ens")
    right, left = lax.rem(gx + 1, n_gx), lax.rem(gx + n_gx - 1, n_gx)
    has_up, has_down = gy > 0, gy < n_gy - 1
    up, down = jnp.maximum(gy - 1, 0), jnp.minimum(gy + 1, n_gy - 1)
    members, rows, cols = state_ref.shape
    patterns = forcing_ref.shape[0]
    fields = patterns + 3
    n_rows = rows + 2 * DEPTH
    n = n_gx * n_gy
    me = gy * n_gx + gx
    peers = [lax.rem(me + o, n) for o in range(1, n)] if reduce_here else []
    where = [{"gx": lax.rem(p, n_gx), "gy": lax.div(p, n_gx)} for p in peers]
    others = [lax.rem(ens + o, n_ens) for o in range(1, n_ens)]

    pairs = [(state_ref.at[:, 0:DEPTH, :], q_lo), (state_ref.at[:, rows - DEPTH:, :], q_hi)]
    for h, dst in ((0, f_lo), (rows - DEPTH, f_hi)):
        pairs += [(forcing_ref.at[:, h:h + DEPTH, :], dst.at[0:patterns]),
                  (u_ref.at[h:h + DEPTH, :], dst.at[patterns]), (v_ref.at[h:h + DEPTH, :], dst.at[patterns + 1])]
    pairs += [(land_ref, land_b), (mode_in, mode_ref), (theta_in, theta_ref), (index_in, index_ref),
              (val_in, val_ref), (sig_in, sig_ref)]
    loads = [pltpu.make_async_copy(s, d, load_sem.at[k]) for k, (s, d) in enumerate(pairs)]
    for c in loads:
        c.start()

    barrier = pltpu.get_barrier_semaphore()

    def greet(dev):
        pl.semaphore_signal(barrier, inc=1, device_id=dev, device_id_type=MESH)

    if reduce_here:
        for d in where:
            greet(d)
        expected = len(where)
    else:
        sides = 2
        expected = sides
        for dev in (right, left):
            greet({"gx": dev})
        for ok, dev in ((has_up, up), (has_down, down)):
            @pl.when(ok)
            def _():
                greet({"gy": dev})
                for other in (right, left):
                    greet({"gx": other, "gy": dev})
            expected = expected + (1 + sides) * ok.astype(I32)
    for p in others:
        greet({"ens": p})
    expected = expected + len(others)

    shape = (8, cols)
    lane = lax.broadcasted_iota(I32, shape, 1)
    sub = lax.broadcasted_iota(I32, shape, 0)
    low = jnp.bitwise_and(lane, 7)
    block0 = lane - low
    block = jnp.right_shift(lane, 3)
    blocks = cols // 8
    bits = [jnp.bitwise_and(lane, k) != 0 for k in (1, 2, 4)]
    first, last = lane < 8, lane >= cols - 8

    def roll(x, k):
        return pltpu.roll(x, k % cols, 1) if k % cols else x

    def gather(x, idx, axis):
        return jnp.take_along_axis(x, idx, axis=axis, mode="promise_in_bounds")

    def skew(xs):
        return [roll(x, v) for v, x in enumerate(xs)]

    def unskew(ys):
        for k, bit in zip((1, 2, 4), bits):
            ys = [jnp.where(bit, ys[(u + k) & 7], ys[u]) for u in range(8)]
        return [roll(ys[-c & 7], -c) for c in range(8)]

    slot = [0]
    queue = {}

    def at_slot(t, fn):
        if t <= slot[0]:
            fn()
        else:
            queue.setdefault(t, []).append(fn)

    def tick():
        slot[0] += 1
        for fn in queue.pop(slot[0], []):
            fn()

    def drain():
        while queue:
            tick()

    LAT = 3

    for c in loads:
        c.wait()
    for h, dst in ((0, f_lo), (rows - DEPTH, f_hi)):
        dst[patterns + 2] = (1 - land_b[h:h + DEPTH, :]).astype(F32)
        dst[fields:] = jnp.zeros((dst.shape[0] - fields, DEPTH, cols), F32)

    pl.semaphore_wait(barrier, expected)

    downs = [rdma(q_hi, qt_ref, row_send.at[0], row_recv.at[0], {"gy": down}),
             rdma(f_hi.at[0:fields], ft_ref.at[0:fields], row_send.at[1], row_recv.at[1], {"gy": down})]
    ups = [rdma(q_lo, qb_ref, row_send.at[2], row_recv.at[2], {"gy": up}),
           rdma(f_lo.at[0:fields], fb_ref.at[0:fields], row_send.at[3], row_recv.at[3], {"gy": up})]
    dests = (right, left)
    fall = [rdma(corner.at[sd, 0], top_ref.at[sd], diag_send.at[sd], diag_recv.at[sd], {"gx": dests[sd], "gy": down})
            for sd in range(2)]
    rise = [rdma(corner.at[sd, 1], bot_ref.at[sd], diag_send.at[2 + sd], diag_recv.at[2 + sd],
                 {"gx": dests[sd], "gy": up}) for sd in range(2)]

    @pl.when(has_down)
    def _():
        for c in downs:
            c.start()

    @pl.when(has_up)
    def _():
        for c in ups:
            c.start()

    half_blocks = blocks // 2
    row_at = [2 * ((b - DEPTH // 2) % half_blocks) + (1 if (b - DEPTH // 2) % blocks >= half_blocks else 0)
              for b in range(blocks)]
    left_half = lane < cols // 2

    def pack_from(lo_ref, hi_ref, base):
        for g in range(lo_ref.shape[0] // 8):
            vals = []
            for r in range(rows):
                ref = flat(lo_ref if r < DEPTH else hi_ref)
                vals.append(ref[pl.ds(g * 8 * DEPTH + r % DEPTH, 8, stride=DEPTH), :])
            moved = [roll(jnp.where(left_half, vals[row_at[(b + 2) % blocks]], vals[row_at[b]]), 8 * b + 8)
                     for b in range(blocks)]
            hi, lo = moved[0], moved[0]
            for b in range(1, blocks):
                hi = jnp.where(block == b, moved[b], hi)
                lo = jnp.where(block == (b + 1) % blocks, moved[b], lo)
            packed.append((hi, lo))
            for sd in range(2):
                pack[sd, base + g * 8:base + g * 8 + 8, :] = packed[-1][sd]

    packed = []
    logical = [jnp.bitwise_and(block + sd, blocks - 1) for sd in range(2)]
    low_half = [jnp.bitwise_and(x, DEPTH // 2) == 0 for x in logical]
    pack_from(q_lo, q_hi, 0)
    pack_from(f_lo, f_hi, members)
    to_right = rdma(pack.at[0], mid_ref.at[0], gx_send.at[0], gx_recv.at[0], {"gx": right})
    to_left = rdma(pack.at[1], mid_ref.at[1], gx_send.at[1], gx_recv.at[1], {"gx": left})
    to_right.start()
    to_left.start()
    for p in range(len(packed) // 2):
        for sd in range(2):
            x, y = packed[2 * p][sd], roll(packed[2 * p + 1][sd], cols // 4)
            corner[sd, 0, p * 8:p * 8 + 8, :] = jnp.where(low_half[sd], x, y)
            corner[sd, 1, p * 8:p * 8 + 8, :] = jnp.where(low_half[sd], y, x)

    @pl.when(has_down)
    def _():
        for c in fall:
            c.start()

    @pl.when(has_up)
    def _():
        for c in rise:
            c.start()

    TH[...] = jnp.zeros_like(TH)
    TH[0:theta_ref.shape[0], 0:members] = theta_ref[...]
    member = low * 8 + sub
    par = [gather(jnp.broadcast_to(TH[k:k + 1, :], shape), member, 1) for k in range(4)]
    diffuse = 0.05 * (1.0 + 0.5 * jnp.tanh(par[0]))
    hyper = 0.005 * (1.0 + 0.5 * jnp.tanh(par[1]))
    keep = 1.0 - 0.05 * (1.0 + 0.5 * jnp.tanh(par[2]))
    gain = par[3]
    mrow = jnp.concatenate([mode_ref[...], jnp.zeros((1, cols - members), I32)], axis=1)
    pattern_of = gather(jnp.broadcast_to(mrow, shape), member, 1)

    def spread(x):
        return [gather(x, block0 + c, 1) for c in range(8)]

    def place(i):
        return i & 1, (i >> 1) % blocks

    def edge_acc():
        return {"l": [jnp.zeros(shape, F32)] * 2, "r": [jnp.zeros(shape, F32)] * 2}

    def inward(acc, i, x0, x7):
        half, j = place(i)
        g = roll(jnp.where(last, x7, x0), 8 * j)

        def put():
            acc["l"][half] = jnp.where(block == j, g, acc["l"][half])
            acc["r"][half] = jnp.where(block == (j - 1) % blocks, g, acc["r"][half])
        at_slot(slot[0] + LAT, put)

    acc_q = edge_acc()

    def enter(ref, fr, base, ok):
        ref, fr = flat(ref), flat(fr)

        def keep_in(x):
            return x if ok is None else jnp.where(ok, x, 0.0)

        def start(k):
            ys = skew([keep_in(ref[pl.ds(v * 8 * DEPTH + k, 8, stride=DEPTH), :]) for v in range(8)])
            zs = spread(keep_in(fr[pl.ds(k, 8, stride=DEPTH), :]))

            def middle():
                os = unskew(ys)
                for c in range(8):
                    FO[base + k, c] = gain * gather(zs[c], pattern_of, 0)

                def end():
                    for c in range(8):
                        Q[0, base + k, c] = os[c]
                    inward(acc_q, base + k, os[0], os[7])
                at_slot(slot[0] + LAT, end)
            at_slot(slot[0] + LAT, middle)

        for k in range(DEPTH):
            start(k)
            tick()
        for f in range(3):
            x = keep_in(fr[(patterns + f) * DEPTH:(patterns + f + 1) * DEPTH, :])
            x = x if f == 2 else 0.5 * x
            zs = spread(x)

            def keep_us(f=f, zs=zs):
                for c, y in enumerate(zs):
                    US[f, c, base:base + DEPTH, :] = y
            at_slot(slot[0] + LAT, keep_us)
            tick()

    enter(q_lo, f_lo, DEPTH, None)
    enter(q_hi, f_hi, DEPTH + rows - DEPTH, None)
    drain()

    @pl.when(has_down)
    def _():
        for c in ups:
            c.wait_recv()

    @pl.when(has_up)
    def _():
        for c in downs:
            c.wait_recv()

    enter(qt_ref, ft_ref, 0, has_up)
    enter(qb_ref, fb_ref, DEPTH + rows, has_down)
    drain()

    to_right.wait_recv()
    to_left.wait_recv()

    @pl.when(has_down)
    def _():
        for c in rise:
            c.wait_recv()

    @pl.when(has_up)
    def _():
        for c in fall:
            c.wait_recv()

    edge_ok, inner = [], []
    quarter = DEPTH // 2
    for side in range(2):
        ok = jnp.where(logical[side] < quarter, has_up.astype(I32),
                       jnp.where(logical[side] >= blocks - quarter, has_down.astype(I32), 1))
        edge_ok.append(ok > 0)
        inner.append((logical[side] >= quarter) & (logical[side] < blocks - quarter))

    def strip(side, g):
        p = g // 2
        mid = mid_ref[side, g * 8:g * 8 + 8, :]
        top, bot = top_ref[side, p * 8:p * 8 + 8, :], bot_ref[side, p * 8:p * 8 + 8, :]
        if g % 2:
            ends = roll(jnp.where(low_half[side], bot, top), -(cols // 4))
        else:
            ends = jnp.where(low_half[side], top, bot)
        even = jnp.where(inner[side], mid, roll(ends, cols // 2))
        odd = jnp.where(inner[side], roll(mid, cols // 2), ends)
        return [jnp.where(edge_ok[side], x, 0.0) for x in (even, odd)]

    scale = jnp.where(sub < 2, 0.5, 1.0)
    for side in range(2):
        both = [strip(side, v) for v in range(8)]
        cells = strip(side, members // 8)
        extra = strip(side, members // 8 + 1)
        for half in range(2):
            def start(side=side, half=half, both=both, cells=cells, extra=extra):
                ys = skew([b[half] for b in both])
                zs = spread(cells[half])
                ws = spread(scale * extra[half])

                def middle():
                    os = unskew(ys)
                    for c in range(8):
                        FH[side, c, half] = gain * gather(zs[c], pattern_of, 0)
                        UH[side, c, half] = ws[c]

                    def end():
                        for c in range(8):
                            H[0, side, c, half] = os[c]
                    at_slot(slot[0] + LAT, end)
                at_slot(slot[0] + LAT, middle)
            at_slot(slot[0] + 2, start)
            tick()
    drain()

    def masked(i, x):
        if i < DEPTH:
            return jnp.where(has_up, x, 0.0)
        if i >= DEPTH + rows:
            return jnp.where(has_down, x, 0.0)
        return x

    def across(x0, x7, get, i):
        half, j = place(i)
        f = roll(jnp.where(block == j, get(0, 7, half), get(1, 0, half)), -8 * j)
        return jnp.where(first, f, roll(x7, 8)), jnp.where(last, f, roll(x0, -8))

    def vertical(get, side, c):
        m, t = get(side, c, 0), get(side, c, 1)
        return (t, roll(t, 8)), (roll(m, -8), m)

    def halo_x(get, acc, side, c, half):
        if c > 0:
            xm = get(side, c - 1, half)
        else:
            xm = acc["r"][half] if side == 1 else jnp.zeros(shape, F32)
        if c < 7:
            xp = get(side, c + 1, half)
        else:
            xp = acc["l"][half] if side == 0 else jnp.zeros(shape, F32)
        return xm, xp

    def live(side, least):
        return range(least, 8) if side == 0 else range(0, 8 - least)

    def advance(s, acc_in):
        src, dst = s % 2, (s + 1) % 2
        lo, hi = 2 * s, n_rows - 2 * s
        final = s == STEPS - 1
        acc_l, acc_out = edge_acc(), edge_acc()
        qh = lambda side, c, half: H[src, side, c, half]
        lh = lambda side, c, half: LH[side, c, half]
        grads, adv, turn1, turn2, hv, lv = {}, {}, {}, {}, {}, {}
        lap_cells = [(0, 7), (1, 0)] if final else [(sd, c) for sd in range(2) for c in live(sd, lo + 1)]
        new_cells = [] if final else [(sd, c) for sd in range(2) for c in live(sd, lo + 2)]

        def halo_rolls():
            for sd, c in lap_cells:
                hv[sd, c] = vertical(qh, sd, c)

        def halo_lap():
            for sd, c in lap_cells:
                for half in range(2):
                    nxt, prv = hv[sd, c][half]
                    xm, xp = halo_x(qh, acc_in, sd, c, half)
                    lap = (nxt + prv) + (xp + xm) - 4.0 * qh(sd, c, half)
                    LH[sd, c, half] = jnp.where(edge_ok[sd], lap, 0.0)
                    if (sd, c) in new_cells:
                        grads[sd, c, half] = (UH[sd, c, half, 0:1] * (xp - xm) + UH[sd, c, half, 1:2] * (nxt - prv))

        def lap_rolls():
            for sd, c in new_cells:
                lv[sd, c] = vertical(lh, sd, c)

        def halo_new():
            for sd, c in new_cells:
                for half in range(2):
                    nxt, prv = lv[sd, c][half]
                    xm, xp = halo_x(lh, acc_l, sd, c, half)
                    mid = lh(sd, c, half)
                    bi = (nxt + prv) + (xp + xm) - 4.0 * mid
                    new = (keep * qh(sd, c, half) + (FH[sd, c, half] - grads[sd, c, half])
                           + (diffuse * mid - hyper * bi))
                    H[dst, sd, c, half] = new * UH[sd, c, half, 2:3]

        def turn_first(i):
            turn1[i] = across(Q[src, i, 0], Q[src, i, 7], qh, i)

        def first_pass(i):
            left, right = turn1.pop(i)
            row = [Q[src, i, c] for c in range(8)]
            laps = []
            for c in range(8):
                xm = row[c - 1] if c else left
                xp = row[c + 1] if c < 7 else right
                up_, dn = Q[src, i + 1, c], Q[src, i - 1, c]
                laps.append(masked(i, (up_ + dn) + (xp + xm) - 4.0 * row[c]))
                L[i, c] = laps[c]
                if lo + 2 <= i < hi - 2:
                    a = US[0, c, i:i + 1, :] * (xp - xm) + US[1, c, i:i + 1, :] * (up_ - dn)
                    adv[i, c] = keep * row[c] + (FO[i, c] - a)
            if not final:
                inward(acc_l, i, laps[0], laps[7])
            if lo + 2 <= i < hi - 2:
                turn2[i] = across(laps[0], laps[7], lh, i)

        def second_pass(i):
            left, right = turn2.pop(i)
            row = [L[i, c] for c in range(8)]
            outs = []
            for c in range(8):
                xm = row[c - 1] if c else left
                xp = row[c + 1] if c < 7 else right
                bi = (L[i + 1, c] + L[i - 1, c]) + (xp + xm) - 4.0 * row[c]
                new = (adv.pop((i, c)) + (diffuse * row[c] - hyper * bi)) * US[2, c, i:i + 1, :]
                outs.append(new)
                if not final:
                    Q[dst, i, c] = new
            if not final:
                inward(acc_out, i, outs[0], outs[7])
                return
            ys = skew(outs)

            def middle():
                xs = unskew(ys)

                def end():
                    r = i - DEPTH
                    ref = flat(out_lo if r < DEPTH else out_hi)
                    for v, x in enumerate(xs):
                        ref[pl.ds(v * 8 * DEPTH + r % DEPTH, 8, stride=DEPTH), :] = x
                at_slot(slot[0] + LAT, end)
            at_slot(slot[0] + LAT, middle)

        halo_rolls()
        for k in range(LAT):
            turn_first(lo + 1 + k)
        while any(fn.__name__ == "put" for fns in queue.values() for fn in fns):
            tick()
        halo_lap()
        lap_rolls()
        for i in range(lo + 1, hi - 1):
            if i + LAT < hi - 1:
                turn_first(i + LAT)
            first_pass(i)
            if lo + 2 <= i < hi - 2:
                at_slot(slot[0] + LAT, functools.partial(second_pass, i))
            tick()
        for _ in range(LAT):
            tick()
        if not final:
            halo_new()
        return acc_out

    acc = acc_q
    for s in range(STEPS):
        acc = advance(s, acc)
    drain()

    index = index_ref[0]
    col = jnp.bitwise_and(index, cols - 1)
    row = jnp.right_shift(index, cols.bit_length() - 1)
    hot = (lax.broadcasted_iota(I32, (cols, cols), 0) == col).astype(jnp.bfloat16)
    row_id = lax.broadcasted_iota(I32, (8, DEPTH, cols), 1)
    dot = functools.partial(jnp.dot, preferred_element_type=F32)
    for g in range(members // 8):
        found = []
        for h, ref in ((0, out_lo), (rows - DEPTH, out_hi)):
            x = flat(ref)[pl.ds(g * 8 * DEPTH, 8 * DEPTH), :]
            x1 = x.astype(jnp.bfloat16)
            rem = x - x1.astype(F32)
            x2 = rem.astype(jnp.bfloat16)
            x3 = (rem - x2.astype(F32)).astype(jnp.bfloat16)
            picked = dot(x1, hot) + (dot(x2, hot) + dot(x3, hot))
            found.append(jnp.where(row_id + h == row[None], picked.reshape(8, DEPTH, cols), 0.0))
        obs_ref[pl.ds(g * 8, 8), :] = jnp.sum(found[0] + found[1], axis=1)

    mine = pl.ds(pl.multiple_of(ens * members, members), members)
    obs_copies, th_copies = [], []
    for k, p in enumerate(others):
        obs_copies.append(rdma(obs_ref, obs_all.at[mine], ens_send.at[2 * k], ens_recv.at[2 * k], {"ens": p}))
        th_copies.append(rdma(theta_ref, th_ref.at[ens], ens_send.at[2 * k + 1], ens_recv.at[2 * k + 1], {"ens": p}))
    for c in obs_copies + th_copies:
        c.start()
    obs_all[mine, :] = obs_ref[...]
    th_ref[ens] = theta_ref[...]
    for c in obs_copies:
        c.wait()

    x = obs_all[...]
    mean = jnp.mean(x, axis=0, keepdims=True)
    inv = 1.0 / sig_ref[0]
    anom = (x - mean) * inv
    d = jnp.broadcast_to((val_ref[0] - mean) * inv, (8, x.shape[1]))
    total = x.shape[0]
    gram = lax.dot_general(jnp.concatenate([anom, d], axis=0), anom, (((1,), (1,)), ((), ())),
                           preferred_element_type=F32, precision=HIGH)

    def finish():
        for c in (to_right, to_left):
            c.wait_send()
        for ok, copies in ((has_down, fall + downs), (has_up, rise + ups)):
            @pl.when(ok)
            def _():
                for c in copies:
                    c.wait_send()
        for c in th_copies:
            c.wait()

    if not reduce_here:
        full_ref[...] = gram
        finish()
        return
    part[...] = gram
    own = total // len(owners)
    spans = [pl.ds(k * own, own + (8 if k == len(owners) - 1 else 0)) for k in range(len(owners))]
    rank = [oy * n_gx + ox for ox, oy in owners]

    def to_owner(k, slot_):
        return rdma(part.at[spans[k]], rs.at[slot_, 0:spans[k].size], rs_send.at[k], rs_recv.at[slot_],
                    {"gx": owners[k][0], "gy": owners[k][1]})

    def from_owner(k, j):
        return rdma(full_ref.at[spans[k]], full_ref.at[spans[k]], ag_send.at[j], ag_recv.at[k], where[j])

    for k in range(len(owners)):
        @pl.when(me != rank[k])
        def _():
            to_owner(k, me).start()
    for k in range(len(owners)):
        @pl.when(me == rank[k])
        def _():
            acc = part[spans[k], :]
            for p in range(n):
                if p != rank[k]:
                    to_owner(k, p).wait_recv()
                    acc = acc + rs[p, 0:spans[k].size, :]
            full_ref[spans[k], :] = acc
            for j in range(len(where)):
                from_owner(k, j).start()
    for k in range(len(owners)):
        @pl.when(me != rank[k])
        def _():
            to_owner(k, me).wait_send()
    finish()
    for k in range(len(owners)):
        @pl.when(me != rank[k])
        def _():
            from_owner(k, 0).wait_recv()

        @pl.when(me == rank[k])
        def _():
            for j in range(len(where)):
                from_owner(k, j).wait_send()


def run_step(mesh, state, forcing, u_vel, v_vel, land, member_mode, theta, obs_index, values, sigma):
    n_gx, n_gy, n_ens = mesh.shape["gx"], mesh.shape["gy"], mesh.shape["ens"]
    members, rows, cols = state.shape
    patterns = forcing.shape[0]
    sites = obs_index.shape[-1]
    params = theta.shape[1]
    nf = -(-(patterns + 3) // 8) * 8
    strips = members + nf
    n_rows = rows + 2 * DEPTH
    total = members * n_ens
    n = n_gx * n_gy
    owners = [(ox, oy) for oy in range(1, n_gy, 2) for ox in sorted({max(n_gx // 2 - 1, 0), n_gx // 2})]
    reduce_here = 0 < n <= 32 and len(owners) > 0 and total % (8 * len(owners)) == 0
    own = total // len(owners) + 8 if reduce_here else 8
    slots = n if reduce_here else 1
    sds = jax.ShapeDtypeStruct
    dma = pltpu.SemaphoreType.DMA
    reg = (8, cols)
    out_lo, out_hi, full, th = pl.pallas_call(
        functools.partial(step_kernel, n_gx, n_gy, n_ens, reduce_here, owners),
        out_shape=[sds((members, DEPTH, cols), F32)] * 2 + [sds((total + 8, total), F32),
                   sds((n_ens, params, members), F32)],
        in_specs=[hspec()] * 10,
        out_specs=[vspec()] * 4,
        scratch_shapes=[VM((members, DEPTH, cols), F32)] * 2 + [VM((nf, DEPTH, cols), F32)] * 2
        + [VM((rows, cols), I32), VM((1, members), I32), VM((params, members), F32), VM((1, 1, sites), I32),
           VM((1, 1, sites), F32), VM((1, 1, sites), F32)]
        + [VM((members, DEPTH, cols), F32)] * 2 + [VM((nf, DEPTH, cols), F32)] * 2
        + [VM((2, strips, cols), F32), VM((2, 2, strips // 2, cols), F32), VM((2, strips, cols), F32)]
        + [VM((2, strips // 2, cols), F32)] * 2
        + [VM((2, n_rows, 8) + reg, F32), VM((n_rows, 8) + reg, F32), VM((n_rows, 8) + reg, F32),
           VM((3, 8, n_rows, cols), F32),
           VM((2, 2, 8, 2) + reg, F32), VM((2, 8, 2) + reg, F32), VM((2, 8, 2) + reg, F32),
           VM((2, 8, 2) + reg, F32), VM(reg, F32)]
        + [VM((members, sites), F32), VM((total, sites), F32), VM((total + 8, total), F32), VM((slots, own, total), F32)]
        + [dma((14,)), dma((4,)), dma((4,)), dma((2,)), dma((2,)), dma((4,)), dma((4,))]
        + [dma((2 * (n_ens - 1),))] * 2 + [dma((slots,))] * 4,
        compiler_params=pltpu.CompilerParams(collective_id=0, has_side_effects=True, vmem_limit_bytes=SPACE),
        name="step",
    )(*[pltpu.with_memory_space_constraint(x, pltpu.HBM) for x in
        (state, forcing, u_vel, v_vel, land, member_mode.reshape(1, members), theta.T, obs_index, values, sigma)])
    if not reduce_here:
        full = lax.psum(full, ("gx", "gy"))
    return out_lo, out_hi, full, th


def solve_kernel(members, full_ref, th_ref, out_ref, xs):
    total = full_ref.shape[1]
    blocks = total // 8
    n_ens, params = th_ref.shape[0], th_ref.shape[1]
    shape = (8, total)
    lane = lax.broadcasted_iota(jnp.int32, shape, 1)
    sub = lax.broadcasted_iota(jnp.int32, shape, 0)
    tht = jnp.concatenate([th_ref[e] for e in range(n_ens)], axis=1)
    spread = tht - jnp.mean(tht, axis=1, keepdims=True)
    xs[...] = jnp.zeros_like(xs)
    xs[0:params, :] = spread
    cols_of = xs[...].T
    A, R = [], []
    for k in range(blocks):
        rows = slice(8 * k, 8 * k + 8)
        A.append(full_ref[rows, :] + jnp.where(lane == sub + 8 * k, float(total - 1), 0.0))
        R.append(cols_of[rows])

    def splat(x):
        return jnp.broadcast_to(x, shape)

    for k in range(blocks):
        rs_, rr = [], []
        d = {}
        for j in range(8):
            row = splat(A[k][j:j + 1])
            rs_.append(row)
            rr.append(splat(R[k][j:j + 1]))
            for i in range(j, 8):
                d[j, i] = splat(row[:, 8 * k + i:8 * k + i + 1])
        inv = []
        for j in range(8):
            inv.append(1.0 / d[j, j])
            for i in range(j + 1, 8):
                m = d[j, i] * inv[j]
                rs_[i] = rs_[i] - m * rs_[j]
                rr[i] = rr[i] - m * rr[j]
                for q in range(i, 8):
                    d[i, q] = d[i, q] - m * d[j, q]
        for i in reversed(range(8)):
            for j in range(i + 1, 8):
                rs_[i] = rs_[i] - d[i, j] * rs_[j]
                rr[i] = rr[i] - d[i, j] * rr[j]
            rs_[i] = rs_[i] * inv[i]
            rr[i] = rr[i] * inv[i]
        a, r = rs_[7], rr[7]
        for j in range(7):
            a = jnp.where(sub == j, rs_[j], a)
            r = jnp.where(sub == j, rr[j], r)
        A[k], R[k] = a, r
        for i in list(range(k + 1, blocks)) + list(range(k)):
            a, r = A[i], R[i]
            for j in range(8):
                c = splat(A[i][:, 8 * k + j:8 * k + j + 1])
                if k + 1 < blocks:
                    a = a - c * rs_[j]
                r = r - c * rr[j]
            A[i], R[i] = a, r
    for k in range(blocks):
        xs[8 * k:8 * k + 8, :] = R[k]
    x = xs[...].T[0:8]
    shift = jnp.sum(x * full_ref[total:total + 1, :], axis=1, keepdims=True)
    new = (jnp.mean(tht, axis=1, keepdims=True) + shift[0:params]) + float(total - 1) * x[0:params]
    ens = lax.axis_index("ens")
    for e in range(n_ens):
        @pl.when(ens == e)
        def _():
            out_ref[...] = new[:, e * members:(e + 1) * members]


def relay_kernel(members, full_ref, th_ref, lo_ref, hi_ref, out_ref, final_ref, xs, sem):
    depth, rows = lo_ref.shape[1], final_ref.shape[1]
    gives = [pltpu.make_async_copy(lo_ref, final_ref.at[:, 0:depth, :], sem.at[0]),
             pltpu.make_async_copy(hi_ref, final_ref.at[:, rows - depth:, :], sem.at[1])]
    for c in gives:
        c.start()
    solve_kernel(members, full_ref, th_ref, out_ref, xs)
    for c in gives:
        c.wait()


def solve(full, th, theta, lo, hi, shape):
    total = full.shape[1]
    out, final = pl.pallas_call(
        functools.partial(relay_kernel, theta.shape[0]),
        out_shape=[jax.ShapeDtypeStruct(theta.shape[::-1], F32), jax.ShapeDtypeStruct(shape, F32)],
        in_specs=[vspec()] * 4,
        out_specs=[vspec(), hspec()],
        scratch_shapes=[VM((total, total), F32), pltpu.SemaphoreType.DMA((2,))],
        compiler_params=pltpu.CompilerParams(vmem_limit_bytes=SMALL_SPACE),
        name="solve",
    )(full, th, lo, hi)
    return out.T, final


def local(mesh, state, u_vel, v_vel, land, forcing, member_mode, theta, obs_index, obs_values, obs_sigma):
    lo, hi, full, th = run_step(mesh, state, forcing, u_vel, v_vel, land, member_mode, theta, obs_index,
                                obs_values, obs_sigma)
    new_theta, final = solve(full, th, theta, lo, hi, state.shape)
    return final, new_theta


def solution(mesh):
    placed = (
        P("ens", "gy", "gx"),
        P("gy", "gx"),
        P("gy", "gx"),
        P("gy", "gx"),
        P(None, "gy", "gx"),
        P("ens"),
        P("ens", None),
        P("gy", "gx", None),
        P("gy", "gx", None),
        P("gy", "gx", None),
    )
    return jax.shard_map(
        functools.partial(local, mesh),
        mesh=mesh,
        in_specs=placed,
        out_specs=(P("ens", "gy", "gx"), P("ens", None)),
        check_vma=False,
    )
```

time: 42.5 us -> 34.7 us (0.82)
  Pallas kernels: 41.6 us -> 33.9 us
    pallas_call x1, Pallas kernels: 34.4 us -> 28.1 us  [run_step(): pl.pallas_call(functools.partial(step_kernel, n_gx, n_gy, n_ens, reduce_h...]
    pallas_call x1, Pallas kernels: 7.24 us -> 5.78 us  [solve(): pl.pallas_call(functools.partial(relay_kernel, theta.shape[0]), out_shape...]
where the time goes in v2:
time: 34.7 us; the launch traced here: 34.5 us
  Pallas kernels  33.9 us (98%)
  between operations  0.64 us (2%)
    pallas_call x1, Pallas kernels, run_step(): pl.pallas_call(functools.partial(step_kernel, n_gx, n_gy, n_ens, reduce_h...  28.1 us
    pallas_call x1, Pallas kernels, solve(): pl.pallas_call(functools.partial(relay_kernel, theta.shape[0]), out_shape...  5.78 us

profile of v2, /device:TPU:0, one launch (start us, length us, event | category | flops | bytes accessed | tf_op | source)
XLA Modules:
  0.0 34.5 jit_solution(16917180433117038033)
XLA Ops:
  0.6 28.1 %step.1 = (f32[64,8,128]{2,1,0:T(8,128)S(1)}, f32[64,8,128]{2,1,0:T(8,128)S(1)}, f32[136,128]{1,0:T(8,128)S(1)}, f32[2,4,64]{2,1,0:T(4,128)S(1)}) custom-call(f32[64,16,128]{2,1,0:T(8,128)} %state_ref.1, f32[8,16,128]{2,1,0:T(8,128)} %forcing_ref.1, f32[16,128]{1,0:T(8,128)} %u_ref.1, f32[16,128]{1,0:T(8,128)} %v_ref.1, s32[16,128]{1,0:T(8,128)} %land_ref.1, ...), custom_call_target="tpu_custom_call" | custom-call | tf_op jit(solution)/shard_map/step/pallas_call | solution.py:620
  28.7 5.8 %solve.1 = (f32[4,64]{1,0:T(4,128)}, f32[64,16,128]{2,1,0:T(8,128)}) custom-call(f32[136,128]{1,0:T(8,128)S(1)} %get-tuple-element.8.full_ref, f32[2,4,64]{2,1,0:T(4,128)S(1)} %get-tuple-element.9.th_ref, f32[64,8,128]{2,1,0:T(8,128)S(1)} %get-tuple-element.10.lo_ref, f32[64,8,128]{2,1,0:T(8,128)S(1)} %get-tuple-element.11.hi_ref), custom_call_target="tpu_custom_call" | custom-call | tf_op jit(solution)/shard_map/solve/pallas_call | solution.py:731

commit v3 on v2

--- a/solution.py
+++ b/solution.py
@@ -148,10 +148,13 @@
 
     pl.semaphore_wait(barrier, expected)
 
-    downs = [rdma(q_hi, qt_ref, row_send.at[0], row_recv.at[0], {"gy": down}),
-             rdma(f_hi.at[0:fields], ft_ref.at[0:fields], row_send.at[1], row_recv.at[1], {"gy": down})]
-    ups = [rdma(q_lo, qb_ref, row_send.at[2], row_recv.at[2], {"gy": up}),
-           rdma(f_lo.at[0:fields], fb_ref.at[0:fields], row_send.at[3], row_recv.at[3], {"gy": up})]
+    half_rows = DEPTH // 2
+    near = [slice(0, half_rows), slice(half_rows, DEPTH)]
+    downs = [rdma(f_hi.at[0:fields], ft_ref.at[0:fields], row_send.at[0], row_recv.at[0], {"gy": down})]
+    ups = [rdma(f_lo.at[0:fields], fb_ref.at[0:fields], row_send.at[3], row_recv.at[3], {"gy": up})]
+    for k, r in enumerate(near):
+        downs.append(rdma(q_hi.at[:, r, :], qt_ref.at[:, r, :], row_send.at[1 + k], row_recv.at[1 + k], {"gy": down}))
+        ups.append(rdma(q_lo.at[:, r, :], qb_ref.at[:, r, :], row_send.at[4 + k], row_recv.at[4 + k], {"gy": up}))
     dests = (right, left)
     fall = [rdma(corner.at[sd, 0], top_ref.at[sd], diag_send.at[sd], diag_recv.at[sd], {"gx": dests[sd], "gy": down})
             for sd in range(2)]
@@ -220,6 +223,7 @@
     par = [gather(jnp.broadcast_to(TH[k:k + 1, :], shape), member, 1) for k in range(4)]
     diffuse = 0.05 * (1.0 + 0.5 * jnp.tanh(par[0]))
     hyper = 0.005 * (1.0 + 0.5 * jnp.tanh(par[1]))
+    lap_gain = diffuse + 4.0 * hyper
     keep = 1.0 - 0.05 * (1.0 + 0.5 * jnp.tanh(par[2]))
     gain = par[3]
     mrow = jnp.concatenate([mode_ref[...], jnp.zeros((1, cols - members), I32)], axis=1)
@@ -245,59 +249,74 @@
 
     acc_q = edge_acc()
 
-    def enter(ref, fr, base, ok):
-        ref, fr = flat(ref), flat(fr)
-
-        def keep_in(x):
-            return x if ok is None else jnp.where(ok, x, 0.0)
-
-        def start(k):
-            ys = skew([keep_in(ref[pl.ds(v * 8 * DEPTH + k, 8, stride=DEPTH), :]) for v in range(8)])
-            zs = spread(keep_in(fr[pl.ds(k, 8, stride=DEPTH), :]))
-
-            def middle():
-                os = unskew(ys)
+    def kept(ok, x):
+        return x if ok is None else jnp.where(ok, x, 0.0)
+
+    def enter_row(ref, k, base, ok):
+        ref = flat(ref)
+        ys = skew([kept(ok, ref[pl.ds(v * 8 * DEPTH + k, 8, stride=DEPTH), :]) for v in range(8)])
+
+        def middle():
+            os = unskew(ys)
+
+            def end():
                 for c in range(8):
-                    FO[base + k, c] = gain * gather(zs[c], pattern_of, 0)
-
-                def end():
-                    for c in range(8):
-                        Q[0, base + k, c] = os[c]
-                    inward(acc_q, base + k, os[0], os[7])
-                at_slot(slot[0] + LAT, end)
-            at_slot(slot[0] + LAT, middle)
-
-        for k in range(DEPTH):
-            start(k)
-            tick()
+                    Q[0, base + k, c] = os[c]
+                inward(acc_q, base + k, os[0], os[7])
+            at_slot(slot[0] + LAT, end)
+        at_slot(slot[0] + LAT, middle)
+
+    def enter_field_row(fr, k, base, ok):
+        zs = spread(kept(ok, flat(fr)[pl.ds(k, 8, stride=DEPTH), :]))
+
+        def end():
+            for c in range(8):
+                FO[base + k, c] = gain * gather(zs[c], pattern_of, 0)
+        at_slot(slot[0] + LAT, end)
+
+    def enter_planes(fr, base, ok):
         for f in range(3):
-            x = keep_in(fr[(patterns + f) * DEPTH:(patterns + f + 1) * DEPTH, :])
+            x = kept(ok, flat(fr)[(patterns + f) * DEPTH:(patterns + f + 1) * DEPTH, :])
             x = x if f == 2 else 0.5 * x
             zs = spread(x)
 
-            def keep_us(f=f, zs=zs):
+            def end(f=f, zs=zs):
                 for c, y in enumerate(zs):
                     US[f, c, base:base + DEPTH, :] = y
-            at_slot(slot[0] + LAT, keep_us)
+            at_slot(slot[0] + LAT, end)
             tick()
 
-    enter(q_lo, f_lo, DEPTH, None)
-    enter(q_hi, f_hi, DEPTH + rows - DEPTH, None)
+    def await_rows(k):
+        @pl.when(has_down)
+        def _():
+            ups[k].wait_recv()
+
+        @pl.when(has_up)
+        def _():
+            downs[k].wait_recv()
+
+    for ref, fr, base in ((q_lo, f_lo, DEPTH), (q_hi, f_hi, rows)):
+        for k in range(DEPTH):
+            enter_row(ref, k, base, None)
+            enter_field_row(fr, k, base, None)
+            tick()
+        enter_planes(fr, base, None)
     drain()
 
-    @pl.when(has_down)
-    def _():
-        for c in ups:
-            c.wait_recv()
-
-    @pl.when(has_up)
-    def _():
-        for c in downs:
-            c.wait_recv()
-
-    enter(qt_ref, ft_ref, 0, has_up)
-    enter(qb_ref, fb_ref, DEPTH + rows, has_down)
+    await_rows(0)
+    for fr, base, ok in ((ft_ref, 0, has_up), (fb_ref, DEPTH + rows, has_down)):
+        for k in range(DEPTH):
+            enter_field_row(fr, k, base, ok)
+            tick()
+        enter_planes(fr, base, ok)
     drain()
+    for part_ in range(len(near)):
+        await_rows(1 + part_)
+        for ref, base, ok in ((qt_ref, 0, has_up), (qb_ref, DEPTH + rows, has_down)):
+            for k in range(near[part_].start, near[part_].stop):
+                enter_row(ref, k, base, ok)
+                tick()
+        drain()
 
     to_right.wait_recv()
     to_left.wait_recv()
@@ -423,9 +442,9 @@
                     nxt, prv = lv[sd, c][half]
                     xm, xp = halo_x(lh, acc_l, sd, c, half)
                     mid = lh(sd, c, half)
-                    bi = (nxt + prv) + (xp + xm) - 4.0 * mid
+                    around = (nxt + prv) + (xp + xm)
                     new = (keep * qh(sd, c, half) + (FH[sd, c, half] - grads[sd, c, half])
-                           + (diffuse * mid - hyper * bi))
+                           + (lap_gain * mid - hyper * around))
                     H[dst, sd, c, half] = new * UH[sd, c, half, 2:3]
 
         def turn_first(i):
@@ -456,8 +475,8 @@
             for c in range(8):
                 xm = row[c - 1] if c else left
                 xp = row[c + 1] if c < 7 else right
-                bi = (L[i + 1, c] + L[i - 1, c]) + (xp + xm) - 4.0 * row[c]
-                new = (adv.pop((i, c)) + (diffuse * row[c] - hyper * bi)) * US[2, c, i:i + 1, :]
+                around = (L[i + 1, c] + L[i - 1, c]) + (xp + xm)
+                new = (adv.pop((i, c)) + (lap_gain * row[c] - hyper * around)) * US[2, c, i:i + 1, :]
                 outs.append(new)
                 if not final:
                     Q[dst, i, c] = new
@@ -634,7 +653,7 @@
            VM((2, 2, 8, 2) + reg, F32), VM((2, 8, 2) + reg, F32), VM((2, 8, 2) + reg, F32),
            VM((2, 8, 2) + reg, F32), VM(reg, F32)]
         + [VM((members, sites), F32), VM((total, sites), F32), VM((total + 8, total), F32), VM((slots, own, total), F32)]
-        + [dma((14,)), dma((4,)), dma((4,)), dma((2,)), dma((2,)), dma((4,)), dma((4,))]
+        + [dma((14,)), dma((6,)), dma((6,)), dma((2,)), dma((2,)), dma((4,)), dma((4,))]
         + [dma((2 * (n_ens - 1),))] * 2 + [dma((slots,))] * 4,
         compiler_params=pltpu.CompilerParams(collective_id=0, has_side_effects=True, vmem_limit_bytes=SPACE),
         name="step",
@@ -666,45 +685,60 @@
     def splat(x):
         return jnp.broadcast_to(x, shape)
 
+    def columns(x, k):
+        return [jnp.take_along_axis(x, jnp.full(shape, 8 * k + j, jnp.int32), axis=1, mode="promise_in_bounds")
+                for j in range(8)]
+
+    def less(x, terms):
+        terms = list(terms)
+        while len(terms) > 1:
+            terms = [sum(terms[t:t + 2][1:], terms[t]) for t in range(0, len(terms), 2)]
+        return x - terms[0]
+
     for k in range(blocks):
-        rs_, rr = [], []
-        d = {}
-        for j in range(8):
-            row = splat(A[k][j:j + 1])
-            rs_.append(row)
-            rr.append(splat(R[k][j:j + 1]))
-            for i in range(j, 8):
-                d[j, i] = splat(row[:, 8 * k + i:8 * k + i + 1])
-        inv = []
-        for j in range(8):
-            inv.append(1.0 / d[j, j])
-            for i in range(j + 1, 8):
-                m = d[j, i] * inv[j]
-                rs_[i] = rs_[i] - m * rs_[j]
-                rr[i] = rr[i] - m * rr[j]
+        cols_k = columns(A[k], k)
+        d = {(j, i): splat(cols_k[i][j:j + 1]) for j in range(8) for i in range(j, 8)}
+        sets = [[splat(A[k][j:j + 1]) for j in range(8)]]
+        if k == 0:
+            sets.append([splat(R[k][j:j + 1]) for j in range(8)])
+        pairs = {}
+        for p in range(0, 8, 2):
+            a, b, c = d[p, p], d[p, p + 1], d[p + 1, p + 1]
+            r = 1.0 / (a * c - b * b)
+            pairs[p] = a * r, b * r, c * r
+            for i in range(p + 2, 8):
+                m0 = (d[p, i] * c - d[p + 1, i] * b) * r
+                m1 = (d[p + 1, i] * a - d[p, i] * b) * r
+                for rs_ in sets:
+                    rs_[i] = rs_[i] - (m0 * rs_[p] + m1 * rs_[p + 1])
                 for q in range(i, 8):
-                    d[i, q] = d[i, q] - m * d[j, q]
-        for i in reversed(range(8)):
-            for j in range(i + 1, 8):
-                rs_[i] = rs_[i] - d[i, j] * rs_[j]
-                rr[i] = rr[i] - d[i, j] * rr[j]
-            rs_[i] = rs_[i] * inv[i]
-            rr[i] = rr[i] * inv[i]
-        a, r = rs_[7], rr[7]
-        for j in range(7):
-            a = jnp.where(sub == j, rs_[j], a)
-            r = jnp.where(sub == j, rr[j], r)
-        A[k], R[k] = a, r
+                    d[i, q] = d[i, q] - (m0 * d[p, q] + m1 * d[p + 1, q])
+        for p in reversed(range(0, 8, 2)):
+            ar, br, cr = pairs[p]
+            for rs_ in sets:
+                y0, y1 = rs_[p], rs_[p + 1]
+                if p < 6:
+                    y0 = less(y0, [d[p, j] * rs_[j] for j in range(p + 2, 8)])
+                    y1 = less(y1, [d[p + 1, j] * rs_[j] for j in range(p + 2, 8)])
+                rs_[p], rs_[p + 1] = cr * y0 - br * y1, ar * y1 - br * y0
+
+        def merge(rs_):
+            x = rs_[7]
+            for j in range(7):
+                x = jnp.where(sub == j, rs_[j], x)
+            return x
+
         for i in list(range(k + 1, blocks)) + list(range(k)):
-            a, r = A[i], R[i]
-            for j in range(8):
-                c = splat(A[i][:, 8 * k + j:8 * k + j + 1])
-                if k + 1 < blocks:
-                    a = a - c * rs_[j]
-                r = r - c * rr[j]
-            A[i], R[i] = a, r
+            c = columns(A[i], k)
+            A[i] = less(A[i], [c[j] * sets[0][j] for j in range(8)])
+            if k == 0:
+                R[i] = less(R[i], [c[j] * sets[1][j] for j in range(8)])
+                A[i] = jnp.where(lane < 8, R[i], A[i])
+        A[k] = merge(sets[0])
+        if k == 0:
+            A[k] = jnp.where(lane < 8, merge(sets[1]), A[k])
     for k in range(blocks):
-        xs[8 * k:8 * k + 8, :] = R[k]
+        xs[8 * k:8 * k + 8, :] = A[k]
     x = xs[...].T[0:8]
     shift = jnp.sum(x * full_ref[total:total + 1, :], axis=1, keepdims=True)
     new = (jnp.mean(tht, axis=1, keepdims=True) + shift[0:params]) + float(total - 1) * x[0:params]

time: 34.7 us -> 32.8 us (0.945)
  Pallas kernels: 33.9 us -> 32 us
    pallas_call x1, Pallas kernels: 5.78 us -> 4.6 us  [solve(): pl.pallas_call(functools.partial(relay_kernel, theta.shape[0]), out_shape...]
    pallas_call x1, Pallas kernels: 28.1 us -> 27.4 us  [run_step(): pl.pallas_call(functools.partial(step_kernel, n_gx, n_gy, n_ens, reduce_h...]
where the time goes in v3:
time: 32.8 us; the launch traced here: 32.6 us
  Pallas kernels  32 us (98%)
  between operations  0.64 us (2%)
    pallas_call x1, Pallas kernels, run_step(): pl.pallas_call(functools.partial(step_kernel, n_gx, n_gy, n_ens, reduce_h...  27.4 us
    pallas_call x1, Pallas kernels, solve(): pl.pallas_call(functools.partial(relay_kernel, theta.shape[0]), out_shape...  4.6 us

profile of v3, /device:TPU:0, one launch (start us, length us, event | category | flops | bytes accessed | tf_op | source)
XLA Modules:
  0.0 32.6 jit_solution(4559966217663829521)
XLA Ops:
  0.6 27.4 %step.1 = (f32[64,8,128]{2,1,0:T(8,128)S(1)}, f32[64,8,128]{2,1,0:T(8,128)S(1)}, f32[136,128]{1,0:T(8,128)S(1)}, f32[2,4,64]{2,1,0:T(4,128)S(1)}) custom-call(f32[64,16,128]{2,1,0:T(8,128)} %state_ref.1, f32[8,16,128]{2,1,0:T(8,128)} %forcing_ref.1, f32[16,128]{1,0:T(8,128)} %u_ref.1, f32[16,128]{1,0:T(8,128)} %v_ref.1, s32[16,128]{1,0:T(8,128)} %land_ref.1, ...), custom_call_target="tpu_custom_call" | custom-call | tf_op jit(solution)/shard_map/step/pallas_call | solution.py:639
  28.0 4.6 %solve.1 = (f32[4,64]{1,0:T(4,128)}, f32[64,16,128]{2,1,0:T(8,128)}) custom-call(f32[136,128]{1,0:T(8,128)S(1)} %get-tuple-element.8.full_ref, f32[2,4,64]{2,1,0:T(4,128)S(1)} %get-tuple-element.9.th_ref, f32[64,8,128]{2,1,0:T(8,128)S(1)} %get-tuple-element.10.lo_ref, f32[64,8,128]{2,1,0:T(8,128)S(1)} %get-tuple-element.11.hi_ref), custom_call_target="tpu_custom_call" | custom-call | tf_op jit(solution)/shard_map/solve/pallas_call | solution.py:765

commit v4 on v3

--- a/solution.py
+++ b/solution.py
@@ -77,8 +77,9 @@
         pl.semaphore_signal(barrier, inc=1, device_id=dev, device_id_type=MESH)
 
     if reduce_here:
-        for d in where:
-            greet(d)
+        order = sorted(range(1, n), key=lambda o: min(o, n - o))
+        for o in order:
+            greet(where[o - 1])
         expected = len(where)
     else:
         sides = 2
@@ -146,8 +147,6 @@
         dst[patterns + 2] = (1 - land_b[h:h + DEPTH, :]).astype(F32)
         dst[fields:] = jnp.zeros((dst.shape[0] - fields, DEPTH, cols), F32)
 
-    pl.semaphore_wait(barrier, expected)
-
     half_rows = DEPTH // 2
     near = [slice(0, half_rows), slice(half_rows, DEPTH)]
     downs = [rdma(f_hi.at[0:fields], ft_ref.at[0:fields], row_send.at[0], row_recv.at[0], {"gy": down})]
@@ -160,16 +159,6 @@
             for sd in range(2)]
     rise = [rdma(corner.at[sd, 1], bot_ref.at[sd], diag_send.at[2 + sd], diag_recv.at[2 + sd],
                  {"gx": dests[sd], "gy": up}) for sd in range(2)]
-
-    @pl.when(has_down)
-    def _():
-        for c in downs:
-            c.start()
-
-    @pl.when(has_up)
-    def _():
-        for c in ups:
-            c.start()
 
     half_blocks = blocks // 2
     row_at = [2 * ((b - DEPTH // 2) % half_blocks) + (1 if (b - DEPTH // 2) % blocks >= half_blocks else 0)
@@ -199,22 +188,35 @@
     pack_from(f_lo, f_hi, members)
     to_right = rdma(pack.at[0], mid_ref.at[0], gx_send.at[0], gx_recv.at[0], {"gx": right})
     to_left = rdma(pack.at[1], mid_ref.at[1], gx_send.at[1], gx_recv.at[1], {"gx": left})
-    to_right.start()
-    to_left.start()
     for p in range(len(packed) // 2):
         for sd in range(2):
             x, y = packed[2 * p][sd], roll(packed[2 * p + 1][sd], cols // 4)
             corner[sd, 0, p * 8:p * 8 + 8, :] = jnp.where(low_half[sd], x, y)
             corner[sd, 1, p * 8:p * 8 + 8, :] = jnp.where(low_half[sd], y, x)
 
+    pl.semaphore_wait(barrier, expected)
+    to_right.start()
+    to_left.start()
+    mine = pl.ds(pl.multiple_of(ens * members, members), members)
+    th_copies, obs_copies = [], []
+    early = members // 16 * 8
+    for k, p in enumerate(others):
+        th_copies.append(rdma(theta_ref, th_ref.at[ens], ens_send.at[3 * k], ens_recv.at[3 * k], {"ens": p}))
+        for h, (at, size) in enumerate(((0, early), (early, members - early))):
+            there = pl.ds(pl.multiple_of(ens * members + at, 8), size)
+            obs_copies.append((h, rdma(obs_ref.at[at:at + size], obs_all.at[there], ens_send.at[3 * k + 1 + h],
+                                       ens_recv.at[3 * k + 1 + h], {"ens": p})))
+    for c in th_copies:
+        c.start()
+
     @pl.when(has_down)
     def _():
-        for c in fall:
+        for c in fall + downs:
             c.start()
 
     @pl.when(has_up)
     def _():
-        for c in rise:
+        for c in rise + ups:
             c.start()
 
     TH[...] = jnp.zeros_like(TH)
@@ -538,17 +540,13 @@
             picked = dot(x1, hot) + (dot(x2, hot) + dot(x3, hot))
             found.append(jnp.where(row_id + h == row[None], picked.reshape(8, DEPTH, cols), 0.0))
         obs_ref[pl.ds(g * 8, 8), :] = jnp.sum(found[0] + found[1], axis=1)
-
-    mine = pl.ds(pl.multiple_of(ens * members, members), members)
-    obs_copies, th_copies = [], []
-    for k, p in enumerate(others):
-        obs_copies.append(rdma(obs_ref, obs_all.at[mine], ens_send.at[2 * k], ens_recv.at[2 * k], {"ens": p}))
-        th_copies.append(rdma(theta_ref, th_ref.at[ens], ens_send.at[2 * k + 1], ens_recv.at[2 * k + 1], {"ens": p}))
-    for c in obs_copies + th_copies:
-        c.start()
+        for h, c in obs_copies:
+            if (g + 1) * 8 == (early, members)[h]:
+                c.start()
+
     obs_all[mine, :] = obs_ref[...]
     th_ref[ens] = theta_ref[...]
-    for c in obs_copies:
+    for _, c in obs_copies:
         c.wait()
 
     x = obs_all[...]
@@ -581,31 +579,40 @@
     rank = [oy * n_gx + ox for ox, oy in owners]
 
     def to_owner(k, slot_):
-        return rdma(part.at[spans[k]], rs.at[slot_, 0:spans[k].size], rs_send.at[k], rs_recv.at[slot_],
+        return rdma(part.at[spans[k]], rs.at[slot_, 0:spans[k].size], rs_send.at[k], rs_recv.at[0],
                     {"gx": owners[k][0], "gy": owners[k][1]})
 
+    def all_slots(k):
+        return rs.at[:, 0:spans[k].size]
+
+    def arrivals(k):
+        return rdma(all_slots(k), all_slots(k), rs_send.at[k], rs_recv.at[0],
+                    {"gx": owners[k][0], "gy": owners[k][1]})
+
+    def departures(k):
+        return rdma(all_slots(k), all_slots(k), ag_send.at[0], ag_recv.at[k], where[0])
+
     def from_owner(k, j):
-        return rdma(full_ref.at[spans[k]], full_ref.at[spans[k]], ag_send.at[j], ag_recv.at[k], where[j])
+        return rdma(full_ref.at[spans[k]], full_ref.at[spans[k]], ag_send.at[0], ag_recv.at[k], where[j])
 
     for k in range(len(owners)):
         @pl.when(me != rank[k])
         def _():
-            to_owner(k, me).start()
+            to_owner(k, lax.rem(me + (n - 1 - rank[k]), n)).start()
     for k in range(len(owners)):
         @pl.when(me == rank[k])
         def _():
-            acc = part[spans[k], :]
-            for p in range(n):
-                if p != rank[k]:
-                    to_owner(k, p).wait_recv()
-                    acc = acc + rs[p, 0:spans[k].size, :]
-            full_ref[spans[k], :] = acc
+            arrivals(k).wait_recv()
+            terms = [part[spans[k], :]] + [rs[p, 0:spans[k].size, :] for p in range(n - 1)]
+            while len(terms) > 1:
+                terms = [sum(terms[t:t + 2][1:], terms[t]) for t in range(0, len(terms), 2)]
+            full_ref[spans[k], :] = terms[0]
             for j in range(len(where)):
                 from_owner(k, j).start()
     for k in range(len(owners)):
         @pl.when(me != rank[k])
         def _():
-            to_owner(k, me).wait_send()
+            to_owner(k, 0).wait_send()
     finish()
     for k in range(len(owners)):
         @pl.when(me != rank[k])
@@ -614,8 +621,7 @@
 
         @pl.when(me == rank[k])
         def _():
-            for j in range(len(where)):
-                from_owner(k, j).wait_send()
+            departures(k).wait_send()
 
 
 def run_step(mesh, state, forcing, u_vel, v_vel, land, member_mode, theta, obs_index, values, sigma):
@@ -632,7 +638,8 @@
     owners = [(ox, oy) for oy in range(1, n_gy, 2) for ox in sorted({max(n_gx // 2 - 1, 0), n_gx // 2})]
     reduce_here = 0 < n <= 32 and len(owners) > 0 and total % (8 * len(owners)) == 0
     own = total // len(owners) + 8 if reduce_here else 8
-    slots = n if reduce_here else 1
+    slots = n - 1 if reduce_here else 1
+    sums = len(owners) if reduce_here else 1
     sds = jax.ShapeDtypeStruct
     dma = pltpu.SemaphoreType.DMA
     reg = (8, cols)
@@ -654,7 +661,7 @@
            VM((2, 8, 2) + reg, F32), VM(reg, F32)]
         + [VM((members, sites), F32), VM((total, sites), F32), VM((total + 8, total), F32), VM((slots, own, total), F32)]
         + [dma((14,)), dma((6,)), dma((6,)), dma((2,)), dma((2,)), dma((4,)), dma((4,))]
-        + [dma((2 * (n_ens - 1),))] * 2 + [dma((slots,))] * 4,
+        + [dma((3 * (n_ens - 1),))] * 2 + [dma((sums,)), dma((1,)), dma((1,)), dma((sums,))],
         compiler_params=pltpu.CompilerParams(collective_id=0, has_side_effects=True, vmem_limit_bytes=SPACE),
         name="step",
     )(*[pltpu.with_memory_space_constraint(x, pltpu.HBM) for x in

time: 32.8 us -> 32.3 us (0.985)
  Pallas kernels: 32 us -> 31.5 us
    pallas_call x1, Pallas kernels: 27.4 us -> 26.9 us  [run_step(): pl.pallas_call(functools.partial(step_kernel, n_gx, n_gy, n_ens, reduce_h...]
where the time goes in v4:
time: 32.3 us; the launch traced here: 32.1 us
  Pallas kernels  31.5 us (98%)
  between operations  0.64 us (2%)
    pallas_call x1, Pallas kernels, run_step(): pl.pallas_call(functools.partial(step_kernel, n_gx, n_gy, n_ens, reduce_h...  26.9 us
    pallas_call x1, Pallas kernels, solve(): pl.pallas_call(functools.partial(relay_kernel, theta.shape[0]), out_shape...  4.6 us

profile of v4, /device:TPU:0, one launch (start us, length us, event | category | flops | bytes accessed | tf_op | source)
XLA Modules:
  0.0 32.1 jit_solution(12566599729740003820)
XLA Ops:
  0.6 26.9 %step.1 = (f32[64,8,128]{2,1,0:T(8,128)S(1)}, f32[64,8,128]{2,1,0:T(8,128)S(1)}, f32[136,128]{1,0:T(8,128)S(1)}, f32[2,4,64]{2,1,0:T(4,128)S(1)}) custom-call(f32[64,16,128]{2,1,0:T(8,128)} %state_ref.1, f32[8,16,128]{2,1,0:T(8,128)} %forcing_ref.1, f32[16,128]{1,0:T(8,128)} %u_ref.1, f32[16,128]{1,0:T(8,128)} %v_ref.1, s32[16,128]{1,0:T(8,128)} %land_ref.1, ...), custom_call_target="tpu_custom_call" | custom-call | tf_op jit(solution)/shard_map/step/pallas_call | solution.py:646
  27.5 4.6 %solve.1 = (f32[4,64]{1,0:T(4,128)}, f32[64,16,128]{2,1,0:T(8,128)}) custom-call(f32[136,128]{1,0:T(8,128)S(1)} %get-tuple-element.8.full_ref, f32[2,4,64]{2,1,0:T(4,128)S(1)} %get-tuple-element.9.th_ref, f32[64,8,128]{2,1,0:T(8,128)S(1)} %get-tuple-element.10.lo_ref, f32[64,8,128]{2,1,0:T(8,128)S(1)} %get-tuple-element.11.hi_ref), custom_call_target="tpu_custom_call" | custom-call | tf_op jit(solution)/shard_map/solve/pallas_call | solution.py:772

commit v5 on v4

--- a/solution.py
+++ b/solution.py
@@ -36,6 +36,39 @@
 def rdma(src, dst, send, recv, dev):
     return pltpu.make_async_remote_copy(src_ref=src, dst_ref=dst, send_sem=send, recv_sem=recv,
                                         device_id=dev, device_id_type=MESH)
+
+
+def folded(total):
+    return total * 5 // 8 + 8
+
+
+def share(size, count):
+    cuts = [8 * (size // 8 * k // count) for k in range(count + 1)]
+    return [pl.ds(a, b - a) for a, b in zip(cuts, cuts[1:])]
+
+
+def fold(g, total):
+    q = total // 4
+    lane = lax.broadcasted_iota(I32, (8, total), 1)
+    rows_of = lambda r: g[r:r + 8]
+    out = [rows_of(r) for r in range(0, q, 8)]
+    for r in range(0, q, 8):
+        out.append(jnp.where(lane < q, pltpu.roll(rows_of(3 * q + r), q, 1), rows_of(q + r)))
+    for r in range(0, q // 2, 8):
+        out.append(jnp.where(lane < 2 * q, pltpu.roll(rows_of(2 * q + q // 2 + r), 2 * q, 1), rows_of(2 * q + r)))
+    return out + [rows_of(total)]
+
+
+def unfold(ref, total):
+    q = total // 4
+    lane = lax.broadcasted_iota(I32, (8, total), 1)
+    rows_of = lambda r: ref[r:r + 8, :]
+    top = [rows_of(r) for r in range(0, q, 8)]
+    second = [rows_of(q + r) for r in range(0, q, 8)]
+    third = [rows_of(2 * q + r) for r in range(0, q // 2, 8)]
+    upper = top + second + third + [pltpu.roll(x, 2 * q, 1) for x in third] + [pltpu.roll(x, 3 * q, 1) for x in second]
+    mirror = jnp.concatenate(upper, axis=0).T
+    return [jnp.where(lane < 8 * k // q * q, mirror[8 * k:8 * k + 8], x) for k, x in enumerate(upper)]
 
 
 def step_kernel(n_gx, n_gy, n_ens, reduce_here, owners,
@@ -139,7 +172,7 @@
         while queue:
             tick()
 
-    LAT = 3
+    LAT = 5
 
     for c in loads:
         c.wait()
@@ -570,12 +603,13 @@
             c.wait()
 
     if not reduce_here:
-        full_ref[...] = gram
+        for k, piece in enumerate(fold(gram, total)):
+            full_ref[8 * k:8 * k + 8, :] = piece
         finish()
         return
-    part[...] = gram
-    own = total // len(owners)
-    spans = [pl.ds(k * own, own + (8 if k == len(owners) - 1 else 0)) for k in range(len(owners))]
+    for k, piece in enumerate(fold(gram, total)):
+        part[8 * k:8 * k + 8, :] = piece
+    spans = share(folded(total), len(owners))
     rank = [oy * n_gx + ox for ox, oy in owners]
 
     def to_owner(k, slot_):
@@ -636,8 +670,8 @@
     total = members * n_ens
     n = n_gx * n_gy
     owners = [(ox, oy) for oy in range(1, n_gy, 2) for ox in sorted({max(n_gx // 2 - 1, 0), n_gx // 2})]
-    reduce_here = 0 < n <= 32 and len(owners) > 0 and total % (8 * len(owners)) == 0
-    own = total // len(owners) + 8 if reduce_here else 8
+    reduce_here = n <= 32 and len(owners) > 0
+    own = max(p.size for p in share(folded(total), len(owners))) if reduce_here else 8
     slots = n - 1 if reduce_here else 1
     sums = len(owners) if reduce_here else 1
     sds = jax.ShapeDtypeStruct
@@ -645,7 +679,7 @@
     reg = (8, cols)
     out_lo, out_hi, full, th = pl.pallas_call(
         functools.partial(step_kernel, n_gx, n_gy, n_ens, reduce_here, owners),
-        out_shape=[sds((members, DEPTH, cols), F32)] * 2 + [sds((total + 8, total), F32),
+        out_shape=[sds((members, DEPTH, cols), F32)] * 2 + [sds((folded(total), total), F32),
                    sds((n_ens, params, members), F32)],
         in_specs=[hspec()] * 10,
         out_specs=[vspec()] * 4,
@@ -659,7 +693,7 @@
            VM((3, 8, n_rows, cols), F32),
            VM((2, 2, 8, 2) + reg, F32), VM((2, 8, 2) + reg, F32), VM((2, 8, 2) + reg, F32),
            VM((2, 8, 2) + reg, F32), VM(reg, F32)]
-        + [VM((members, sites), F32), VM((total, sites), F32), VM((total + 8, total), F32), VM((slots, own, total), F32)]
+        + [VM((members, sites), F32), VM((total, sites), F32), VM((folded(total), total), F32), VM((slots, own, total), F32)]
         + [dma((14,)), dma((6,)), dma((6,)), dma((2,)), dma((2,)), dma((4,)), dma((4,))]
         + [dma((3 * (n_ens - 1),))] * 2 + [dma((sums,)), dma((1,)), dma((1,)), dma((sums,))],
         compiler_params=pltpu.CompilerParams(collective_id=0, has_side_effects=True, vmem_limit_bytes=SPACE),
@@ -684,9 +718,10 @@
     xs[0:params, :] = spread
     cols_of = xs[...].T
     A, R = [], []
+    gram = unfold(full_ref, total)
     for k in range(blocks):
         rows = slice(8 * k, 8 * k + 8)
-        A.append(full_ref[rows, :] + jnp.where(lane == sub + 8 * k, float(total - 1), 0.0))
+        A.append(gram[k] + jnp.where(lane == sub + 8 * k, float(total - 1), 0.0))
         R.append(cols_of[rows])
 
     def splat(x):
@@ -747,7 +782,7 @@
     for k in range(blocks):
         xs[8 * k:8 * k + 8, :] = A[k]
     x = xs[...].T[0:8]
-    shift = jnp.sum(x * full_ref[total:total + 1, :], axis=1, keepdims=True)
+    shift = jnp.sum(x * full_ref[folded(total) - 8:folded(total) - 7, :], axis=1, keepdims=True)
     new = (jnp.mean(tht, axis=1, keepdims=True) + shift[0:params]) + float(total - 1) * x[0:params]
     ens = lax.axis_index("ens")
     for e in range(n_ens):

time: 32.3 us -> 32.1 us (level)
  no operation moved by 1% of the time
where the time goes in v5:
time: 32.1 us; the launch traced here: 31.9 us
  Pallas kernels  31.3 us (98%)
  between operations  0.64 us (2%)
    pallas_call x1, Pallas kernels, run_step(): pl.pallas_call(functools.partial(step_kernel, n_gx, n_gy, n_ens, reduce_h...  26.6 us
    pallas_call x1, Pallas kernels, solve(): pl.pallas_call(functools.partial(relay_kernel, theta.shape[0]), out_shape...  4.7 us

profile of v5, /device:TPU:0, one launch (start us, length us, event | category | flops | bytes accessed | tf_op | source)
XLA Modules:
  0.0 31.9 jit_solution(12700500199349702422)
XLA Ops:
  0.6 26.6 %step.1 = (f32[64,8,128]{2,1,0:T(8,128)S(1)}, f32[64,8,128]{2,1,0:T(8,128)S(1)}, f32[88,128]{1,0:T(8,128)S(1)}, f32[2,4,64]{2,1,0:T(4,128)S(1)}) custom-call(f32[64,16,128]{2,1,0:T(8,128)} %state_ref.1, f32[8,16,128]{2,1,0:T(8,128)} %forcing_ref.1, f32[16,128]{1,0:T(8,128)} %u_ref.1, f32[16,128]{1,0:T(8,128)} %v_ref.1, s32[16,128]{1,0:T(8,128)} %land_ref.1, ...), custom_call_target="tpu_custom_call" | custom-call | tf_op jit(solution)/shard_map/step/pallas_call | solution.py:680
  27.2 4.7 %solve.1 = (f32[4,64]{1,0:T(4,128)}, f32[64,16,128]{2,1,0:T(8,128)}) custom-call(f32[88,128]{1,0:T(8,128)S(1)} %get-tuple-element.8.full_ref, f32[2,4,64]{2,1,0:T(4,128)S(1)} %get-tuple-element.9.th_ref, f32[64,8,128]{2,1,0:T(8,128)S(1)} %get-tuple-element.10.lo_ref, f32[64,8,128]{2,1,0:T(8,128)S(1)} %get-tuple-element.11.hi_ref), custom_call_target="tpu_custom_call" | custom-call | tf_op jit(solution)/shard_map/solve/pallas_call | solution.py:807
